TPU v7x, 32 devices: a whole 2x2x4 slice. The times are simulated.
32 devices in a mesh: sub: 4 (over z), ma: 8 (over y, x, core).
Axes of the slice: x: 2, y: 2, z: 4, core: 2. Of those that a mesh axis runs over, the one named last changes fastest.
Arguments:
- forcing: float32 [2, 256, 2, 64, 512], P(None, 'sub', None, 'ma'), may hold values from -24 to 24
- slot_wavenumber: int32 [64], P('ma'), may hold values from 0 to 511, as said below
- inverse: float32 [4, 2, 64, 64, 512], P('sub'), may hold values from -2 to 2
- edge_weights: float32 [4, 2, 64], P('sub'), may hold values from -1357 to 1357, as said below
Outputs:
- transform_field: float32 [2, 256, 2, 64, 512], P(None, ('sub', 'ma'))
Inputs may be any that keep to these rules, and one draw needn't show every extreme that they name: `slot_wavenumber`: each device's slots hold 4 pairs: slots 2j and 2j + 1 carry a wavenumber m below 256 and 511 - m, in that order; no wavenumber appears twice. `edge_weights`: together with inverse it makes every row of the interface system strictly diagonally dominant with a positive diagonal.
All inputs are finite; a program needn't handle non-finite values.
Results may differ from a plain program's by a relative error of at most 0.0003.
Values sent between devices are 32-bit elements; how exact they have to be, the bound alone decides.
A program may use at most 192 MiB of HBM per device.

v0:
```python
import functools

import jax
import jax.numpy as jnp
from jax import lax
from jax.experimental import pallas as pl
from jax.experimental.pallas import tpu as pltpu
from jax.sharding import PartitionSpec as P

LANES = 128
ROWS = 8
F32 = jnp.float32
MESH = pl.DeviceIdType.MESH
FIRST = 2
VMEM_BYTES = 60 * 1024 * 1024
EARLY = 2


def grid_iotas():
    row = lax.broadcasted_iota(jnp.int32, (ROWS, LANES), 0)
    lane = lax.broadcasted_iota(jnp.int32, (ROWS, LANES), 1)
    return row, lane


def lane_gather(values, index):
    return jnp.take_along_axis(values, index, axis=1, mode="promise_in_bounds")


def solve_kernel(
    dims, slot, edge, forcing, inverse, landed, values_landed, cols,
    raw, blocks_in, even_src, odd_src, part, weighed, packed, ends, everyone, values,
    raw_sem, in_sem, z_send, z_recv, p_send, p_recv, u_send, u_recv, f_send, f_recv, own_sem,
):
    fields, points, degrees, group, subs, groups = dims
    tiles = degrees // LANES
    half = tiles // 2
    wide = tiles + half
    blocks = points // ROWS
    base = 2 * fields * wide
    sub = lax.axis_index("sub")
    me = lax.axis_index("ma")
    row, lane = grid_iotas()
    is_even = (row & 1) == 0

    def target(i):
        return lax.rem(me + lax.rem(i + FIRST, groups), groups)

    def fetch(i):
        return pltpu.make_async_copy(
            inverse.at[0, :, pl.ds(target(i) * group, group)], blocks_in.at[i], in_sem.at[i]
        )

    def send(i):
        return pltpu.make_async_remote_copy(
            src_ref=packed.at[i], dst_ref=landed.at[me],
            send_sem=p_send.at[i], recv_sem=p_recv.at[i],
            device_id=(sub, target(i)), device_id_type=MESH,
        )

    pair = me + 1 - 2 * lax.rem(me, 2)
    senders = [lax.rem(me + groups - k, groups) for k in range(0, groups, 2)]

    def send_values(k):
        to = pair if k == 0 else lax.rem(me + k, groups)
        return pltpu.make_async_remote_copy(
            src_ref=values, dst_ref=values_landed.at[me],
            send_sem=u_send.at[k // 2], recv_sem=u_recv.at[k // 2],
            device_id=(sub, to), device_id_type=MESH,
        )

    def forward(k):
        block = values_landed.at[senders[k // 2]]
        return pltpu.make_async_remote_copy(
            src_ref=block, dst_ref=block,
            send_sem=f_send.at[k // 2], recv_sem=f_recv.at[k // 2],
            device_id=(sub, pair), device_id_type=MESH,
        )

    others = [i for i in range(groups) if (i + FIRST) % groups != 0]
    mine = groups - FIRST
    load = pltpu.make_async_copy(forcing, raw, raw_sem.at[0])
    load.start()
    fetch(0).start()
    barrier = pltpu.get_barrier_semaphore()
    subs_to = [lax.rem(sub + k, subs) for k in range(1, subs)]
    for other in subs_to:
        pl.semaphore_signal(barrier, inc=1, device_id=(other, me), device_id_type=MESH)
    for i in others:
        pl.semaphore_signal(barrier, inc=1, device_id=(sub, target(i)), device_id_type=MESH)

    m = jnp.zeros((ROWS, LANES), jnp.int32)
    for j in range(ROWS // 2):
        m = jnp.where((row >> 1) == j, slot[2 * j], m)
    load.wait()
    for i in range(1, groups):
        fetch(i).start()

    def prepare(q, _):
        inside = jnp.where((q > 0) & (q < points - 1), 1.0, 0.0).astype(F32)
        for f in range(fields):
            for t in range(tiles):
                at = pl.ds(t * LANES, LANES)
                a = raw[f, q, 0, :, at] * inside
                b = raw[f, q, 1, :, at] * inside
                degree = lane + t * LANES
                mixed = jnp.where(is_even, a, pltpu.roll(b, 1, 0))
                even_src[f, q, t] = jnp.where(degree >= m, mixed, 0.0)
                if t >= half:
                    mixed = jnp.where(is_even, pltpu.roll(a, ROWS - 1, 0), b)
                    odd_src[f, q, t - half] = jnp.where(degree >= degrees - 1 - m, mixed, 0.0)
        return 0

    lax.fori_loop(0, points, prepare, 0)
    pl.semaphore_wait(barrier, subs + groups - 2)

    shift_index = (lane - m) & (LANES - 1)
    left_index = (degrees - 1 - m) & (LANES - 1)

    def solve_group(i):
        left = jnp.zeros((ROWS, LANES), F32)
        for f in range(fields):
            for t in range(tiles):
                at = pl.ds(t * LANES, LANES)
                both = t >= half

                def step(block, sums, f=f, t=t, at=at, both=both):
                    sums = list(sums)
                    for r in range(ROWS):
                        q = block * ROWS + r
                        even = even_src[f, q, t]
                        odd = odd_src[f, q, t - half] if both else None
                        for p in range(group):
                            line = blocks_in[i, f, p, block, pl.ds(r, 1), at]
                            entry = jnp.broadcast_to(line, (ROWS, LANES))
                            sums[p] += entry * even
                            if both:
                                sums[group + p] += entry * odd
                    return tuple(sums)

                count = group * (2 if both else 1)
                start = tuple(jnp.zeros((ROWS, LANES), F32) for _ in range(count))
                sums = lax.fori_loop(0, blocks, step, start)
                for p in range(group):
                    part[p, t] = sums[p]
                    if both:
                        part[p, tiles + t - half] = sums[group + p]
            for p in range(group):
                k = f * group + p
                near, far = part[p, tiles], part[p, tiles + 1]
                near_moved = lane_gather(near, shift_index)
                far_moved = lane_gather(far, shift_index)
                packed[i, k * tiles] = jnp.where(
                    lane >= m, part[p, 0], jnp.where(lane - m >= -LANES, far_moved, near_moved)
                )
                packed[i, k * tiles + 1] = jnp.where(lane + LANES >= m, part[p, 1], far_moved)
                packed[i, k * tiles + 2] = part[p, 2]
                packed[i, k * tiles + 3] = part[p, 3]
                spare = jnp.where(
                    m < LANES, lane_gather(far, left_index), lane_gather(near, left_index)
                )
                left = jnp.where(lane == k, spare, left)
        packed[i, fields * group * tiles] = left
        packed[i, fields * group * tiles + 1] = m.astype(F32)

    own = pltpu.make_async_copy(packed.at[mine], landed.at[me], own_sem.at[0])

    def early(i, _):
        fetch(i).wait()
        solve_group(i)
        send(i).start()
        return 0

    lax.fori_loop(0, EARLY, early, 0)
    for i in range(EARLY, groups):
        fetch(i).wait()

    def weigh(block, _):
        for f in range(fields):
            def add(i, sums, f=f):
                sums = list(sums)
                for p in range(group):
                    low = edge[0, 0, target(i) * group + p]
                    top = edge[0, 1, target(i) * group + p]
                    for t in range(tiles):
                        entry = blocks_in[i, f, p, block, :, pl.ds(t * LANES, LANES)]
                        sums[t] += low * entry
                        sums[tiles + t] += top * entry
                return tuple(sums)

            start = tuple(jnp.zeros((ROWS, LANES), F32) for _ in range(2 * tiles))
            sums = lax.fori_loop(0, groups, add, start)
            for t in range(tiles):
                weighed[0, f, block, t] = sums[t]
                weighed[1, f, block, t] = sums[tiles + t]
        return 0

    lax.fori_loop(0, blocks, weigh, 0)
    for f in range(fields):
        def slope_step(block, sums, f=f):
            sums = list(sums)
            for r in range(ROWS):
                q = block * ROWS + r
                for e in range(2):
                    for t in range(tiles):
                        line = weighed[e, f, block, t, pl.ds(r, 1), :]
                        entry = jnp.broadcast_to(line, (ROWS, LANES))
                        sums[e * wide + t] += entry * even_src[f, q, t]
                        if t >= half:
                            sums[e * wide + t + half] += entry * odd_src[f, q, t - half]
            return tuple(sums)

        start = tuple(jnp.zeros((ROWS, LANES), F32) for _ in range(2 * wide))
        sums = lax.fori_loop(0, blocks, slope_step, start)
        for e in range(2):
            for t in range(wide):
                ends[(e * fields + f) * wide + t] = sums[e * wide + t]
            for w in range(2):
                for t in range(wide):
                    source = t if t < tiles else t - half
                    line = weighed[e, f, w * (blocks - 1), source, pl.ds(w * (ROWS - 1), 1), :]
                    ends[base + t, pl.ds(f * 4 + e * 2 + w, 1), :] = line

    z_copies = []
    for i, other in enumerate(subs_to):
        copy = pltpu.make_async_remote_copy(
            src_ref=ends, dst_ref=everyone.at[sub], send_sem=z_send.at[i], recv_sem=z_recv.at[i],
            device_id=(other, me), device_id_type=MESH,
        )
        copy.start()
        z_copies.append(copy)
    everyone[sub] = ends[...]

    def late(i, _):
        solve_group(i)

        @pl.when(i != mine)
        def _():
            send(i).start()

        @pl.when(i == mine)
        def _():
            own.start()

        return 0

    lax.fori_loop(EARLY, groups, late, 0)
    for f in range(fields):
        for p in range(group):
            cols[0, f, pl.ds(p, 1), :] = blocks_in[mine, f, p, 0, pl.ds(0, 1), :]
            cols[1, f, pl.ds(p, 1), :] = blocks_in[mine, f, p, blocks - 1, pl.ds(ROWS - 1, 1), :]
    for copy in z_copies:
        copy.wait()

    for f in range(fields):
        for t in range(wide):
            def influence(s, e, w):
                line = everyone[s, base + t, pl.ds(f * 4 + e * 2 + w, 1), :]
                return jnp.broadcast_to(line, (ROWS, LANES))

            def slope(s, e):
                return everyone[s, (e * fields + f) * wide + t]

            zero = jnp.zeros((ROWS, LANES), F32)
            ratio, reduced = zero, zero
            ratios, reduceds = [], []
            for k in range(subs - 1):
                low = influence(k, 1, 0)
                middle = influence(k, 1, 1) - influence(k + 1, 0, 0)
                up = -influence(k + 1, 0, 1)
                right = slope(k + 1, 0) - slope(k, 1)
                pivot = middle - low * ratio
                reduced = (right - low * reduced) / pivot
                ratio = up / pivot
                ratios.append(ratio)
                reduceds.append(reduced)
            later = zero
            lower_value, upper_value = zero, zero
            for k in range(subs - 2, -1, -1):
                later = reduceds[k] - ratios[k] * later
                lower_value = jnp.where(sub == k + 1, later, lower_value)
                upper_value = jnp.where(sub == k, later, upper_value)
            values[f * wide + t] = lower_value
            values[(fields + f) * wide + t] = upper_value

    for k in list(range(2, groups, 2)) + [0]:
        send_values(k).start()
    own_values = pltpu.make_async_copy(values, values_landed.at[me], own_sem.at[1])
    own_values.start()
    for k in range(2, groups, 2):
        send_values(k).wait_recv()
        forward(k).start()
    own.wait()
    own_values.wait()
    for i in others:
        send(i).wait()
    send_values(0).wait()
    for k in range(2, groups, 2):
        send_values(k).wait_send()
        forward(k).wait()


def finish_kernel(
    dims, landed_in, values_in, cols, result, landed, values, out, landed_sem, values_sem, out_sem
):
    fields, degrees, group, groups = dims
    tiles = degrees // LANES
    half = tiles // 2
    wide = tiles + half

    def take(d):
        return pltpu.make_async_copy(landed_in.at[d], landed.at[d], landed_sem.at[d])

    def take_values(d):
        return pltpu.make_async_copy(values_in.at[d], values.at[d], values_sem.at[d])

    def put(d):
        rows = pl.ds(pl.multiple_of(d * ROWS, ROWS), ROWS)
        return pltpu.make_async_copy(out.at[d], result.at[:, :, :, rows, :], out_sem.at[d])

    for d in range(groups):
        take(d).start()
        take_values(d).start()
    row, lane = grid_iotas()
    is_even = (row & 1) == 0

    def unpack(d, _):
        take(d).wait()
        take_values(d).wait()
        count = fields * group * tiles
        left = landed[d, count]
        m = landed[d, count + 1].astype(jnp.int32)
        back_index = (lane + m) & (LANES - 1)
        for f in range(fields):
            for p in range(group):
                k = f * group + p
                pieces = [landed[d, k * tiles + t] for t in range(tiles)]
                first = lane_gather(pieces[0], back_index)
                second = lane_gather(pieces[1], back_index)
                spare = lane_gather(left, jnp.full((ROWS, LANES), k, jnp.int32))
                even = [
                    jnp.where(lane >= m, pieces[0], 0.0),
                    jnp.where(lane + LANES >= m, pieces[1], 0.0),
                    pieces[2],
                    pieces[3],
                ]
                odd = [None] * half
                moved = [first, jnp.where(lane + m < 2 * LANES, first, second)]
                for t in range(half):
                    degree = lane + (half + t) * LANES
                    odd[t] = jnp.where(
                        degree >= degrees - m,
                        moved[t],
                        jnp.where(degree == degrees - 1 - m, spare, 0.0),
                    )
                for t in range(tiles):
                    at = pl.ds(t * LANES, LANES)
                    low = jnp.broadcast_to(cols[0, f, pl.ds(p, 1), at], (ROWS, LANES))
                    top = jnp.broadcast_to(cols[1, f, pl.ds(p, 1), at], (ROWS, LANES))
                    e = even[t] + values[d, f * wide + t] * low
                    e = e + values[d, (fields + f) * wide + t] * top
                    o = jnp.zeros((ROWS, LANES), F32)
                    if t >= half:
                        spot = tiles + t - half
                        o = odd[t - half] + values[d, f * wide + spot] * low
                        o = o + values[d, (fields + f) * wide + spot] * top
                    out[d, f, p, 0, :, at] = jnp.where(is_even, e, pltpu.roll(o, 1, 0))
                    out[d, f, p, 1, :, at] = jnp.where(is_even, pltpu.roll(e, ROWS - 1, 0), o)
        put(d).start()
        return 0

    lax.fori_loop(0, groups, unpack, 0)
    for d in range(groups):
        put(d).wait()


def body(forcing, slot_wavenumber, inverse, edge_weights):
    fields, points, halves, slots, degrees = forcing.shape
    subs, groups = lax.axis_size("sub"), lax.axis_size("ma")
    group = points // groups
    tiles = degrees // LANES
    half = tiles // 2
    wide = tiles + half
    assert halves == 2 and slots == ROWS and tiles == 4
    count = fields * group * tiles + 2
    end_count = 2 * fields * wide + wide
    value_count = 2 * fields * wide
    shape = jax.ShapeDtypeStruct
    blocks = points // ROWS
    landed, values, cols = pl.pallas_call(
        functools.partial(solve_kernel, (fields, points, degrees, group, subs, groups)),
        in_specs=[
            pl.BlockSpec(memory_space=pltpu.SMEM),
            pl.BlockSpec(memory_space=pltpu.SMEM),
            pl.BlockSpec(memory_space=pl.ANY),
            pl.BlockSpec(memory_space=pl.ANY),
        ],
        out_specs=[
            pl.BlockSpec(memory_space=pl.ANY),
            pl.BlockSpec(memory_space=pl.ANY),
            pl.BlockSpec(memory_space=pltpu.VMEM),
        ],
        out_shape=[
            shape((groups, count, ROWS, LANES), F32),
            shape((groups, value_count, ROWS, LANES), F32),
            shape((2, fields, group, degrees), F32),
        ],
        scratch_shapes=[
            pltpu.VMEM((fields, points, halves, slots, degrees), F32),
            pltpu.VMEM((groups, fields, group, blocks, ROWS, degrees), F32),
            pltpu.VMEM((fields, points, tiles, ROWS, LANES), F32),
            pltpu.VMEM((fields, points, half, ROWS, LANES), F32),
            pltpu.VMEM((group, wide, ROWS, LANES), F32),
            pltpu.VMEM((2, fields, blocks, tiles, ROWS, LANES), F32),
            pltpu.VMEM((groups, count, ROWS, LANES), F32),
            pltpu.VMEM((end_count, ROWS, LANES), F32),
            pltpu.VMEM((subs, end_count, ROWS, LANES), F32),
            pltpu.VMEM((value_count, ROWS, LANES), F32),
            pltpu.SemaphoreType.DMA((1,)),
            pltpu.SemaphoreType.DMA((groups,)),
            pltpu.SemaphoreType.DMA((subs - 1,)),
            pltpu.SemaphoreType.DMA((subs - 1,)),
            pltpu.SemaphoreType.DMA((groups,)),
            pltpu.SemaphoreType.DMA((groups,)),
            pltpu.SemaphoreType.DMA((groups // 2,)),
            pltpu.SemaphoreType.DMA((groups // 2,)),
            pltpu.SemaphoreType.DMA((groups // 2,)),
            pltpu.SemaphoreType.DMA((groups // 2,)),
            pltpu.SemaphoreType.DMA((2,)),
        ],
        compiler_params=pltpu.CompilerParams(
            collective_id=0, has_side_effects=True, vmem_limit_bytes=VMEM_BYTES
        ),
    )(
        slot_wavenumber,
        edge_weights,
        forcing,
        inverse.reshape(1, fields, points, blocks, ROWS, degrees),
    )

    return pl.pallas_call(
        functools.partial(finish_kernel, (fields, degrees, group, groups)),
        in_specs=[
            pl.BlockSpec(memory_space=pl.ANY),
            pl.BlockSpec(memory_space=pl.ANY),
            pl.BlockSpec(memory_space=pltpu.VMEM),
        ],
        out_specs=pl.BlockSpec(memory_space=pl.ANY),
        out_shape=shape((fields, group, halves, slots * groups, degrees), F32),
        scratch_shapes=[
            pltpu.VMEM((groups, count, ROWS, LANES), F32),
            pltpu.VMEM((groups, value_count, ROWS, LANES), F32),
            pltpu.VMEM((groups, fields, group, halves, slots, degrees), F32),
            pltpu.SemaphoreType.DMA((groups,)),
            pltpu.SemaphoreType.DMA((groups,)),
            pltpu.SemaphoreType.DMA((groups,)),
        ],
        compiler_params=pltpu.CompilerParams(vmem_limit_bytes=VMEM_BYTES),
    )(landed, values, cols)


def solution(mesh):
    return jax.shard_map(
        body,
        mesh=mesh,
        in_specs=(
            P(None, "sub", None, "ma", None),
            P("ma"),
            P("sub", None, None, None, None),
            P("sub", None, None),
        ),
        out_specs=P(None, ("sub", "ma"), None, None, None),
        check_vma=False,
    )
```

profile of v0, /device:TPU:3, one launch (start us, length us, event | category | flops | bytes accessed | tf_op | source)
XLA Modules:
  0.0 49.5 jit_solution(4856688220800435425)
XLA Ops:
  0.0 45.3 %shard_map.46 = (f32[8,66,8,128]{3,2,1,0:T(8,128)}, f32[8,24,8,128]{3,2,1,0:T(8,128)}, f32[2,2,8,512]{3,2,1,0:T(8,128)}) custom-call(s32[8]{0:T(128)} %slot.1, f32[1,2,64]{2,1,0:T(2,128)} %edge.1, f32[2,64,2,8,512]{4,3,2,1,0:T(8,128)} %forcing.1, f32[1,2,64,8,8,512]{5,4,3,2,1,0:T(8,128)} %bitcast.1), custom_call_target="tpu_custom_call" | custom-call | tf_op jit(solution)/shard_map/pallas_call | solution.py:389
  45.3 4.2 %shard_map.47 = f32[2,8,2,64,512]{4,3,2,1,0:T(8,128)} custom-call(f32[8,66,8,128]{3,2,1,0:T(8,128)} %get-tuple-element.8.landed_in, f32[8,24,8,128]{3,2,1,0:T(8,128)} %get-tuple-element.9.values_in, f32[2,2,8,512]{3,2,1,0:T(8,128)} %get-tuple-element.10.cols), custom_call_target="tpu_custom_call" | custom-call | tf_op jit(solution)/shard_map/pallas_call | solution.py:440
where the time goes:
time: 49.7 us; the launch traced here: 49.5 us
  Pallas kernels  49.4 us (99%)
    pallas_call x1, Pallas kernels, body(): pl.pallas_call(functools.partial(solve_kernel, (fields, points, degrees,...  45.3 us
    pallas_call x1, Pallas kernels, body(): pl.pallas_call(functools.partial(finish_kernel, (fields, degrees, group,...  4.16 us

commit v1 on v0

v1 whole, which is shorter than its diff:
```python
import functools

import jax
import jax.numpy as jnp
from jax import lax
from jax.experimental import pallas as pl
from jax.experimental.pallas import tpu as pltpu
from jax.sharding import PartitionSpec as P

LANES = 128
ROWS = 8
F32 = jnp.float32
MESH = pl.DeviceIdType.MESH
MARK = 64
VMEM_BYTES = 40 * 1024 * 1024


def grid_iotas():
    row = lax.broadcasted_iota(jnp.int32, (ROWS, LANES), 0)
    lane = lax.broadcasted_iota(jnp.int32, (ROWS, LANES), 1)
    return row, lane


def lane_gather(values, index):
    return jnp.take_along_axis(values, index, axis=1, mode="promise_in_bounds")


def spread(values, k):
    return lane_gather(values, jnp.full((ROWS, LANES), k, jnp.int32))


def exclusive_or(a, b, groups):
    total = 0
    bit = 1
    while bit < groups:
        total = total + lax.rem(a // bit + b // bit, 2) * bit
        bit *= 2
    return total


def pack(pieces, m, degrees):
    _, lane = grid_iotas()
    shift_index = (lane - m) & (LANES - 1)
    left_index = (degrees - 1 - m) & (LANES - 1)
    near, far = pieces[4], pieces[5]
    near_moved = lane_gather(near, shift_index)
    far_moved = lane_gather(far, shift_index)
    first = jnp.where(
        lane >= m, pieces[0], jnp.where(lane - m >= -LANES, far_moved, near_moved)
    )
    second = jnp.where(lane + LANES >= m, pieces[1], far_moved)
    spare = jnp.where(m < LANES, lane_gather(far, left_index), lane_gather(near, left_index))
    return [first, second, pieces[2], pieces[3]], spare


def unpack(pieces, spare, m, degrees):
    _, lane = grid_iotas()
    back_index = (lane + m) & (LANES - 1)
    first = lane_gather(pieces[0], back_index)
    second = lane_gather(pieces[1], back_index)
    moved = [first, jnp.where(lane + m < 2 * LANES, first, second)]
    odd = []
    for t in range(2):
        degree = lane + (2 + t) * LANES
        odd.append(
            jnp.where(
                degree >= degrees - m,
                moved[t],
                jnp.where(degree == degrees - 1 - m, spare, 0.0),
            )
        )
    even = [
        jnp.where(lane >= m, pieces[0], 0.0),
        jnp.where(lane + LANES >= m, pieces[1], 0.0),
        pieces[2],
        pieces[3],
    ]
    return even + odd


def solve_kernel(
    dims, slot, edge, forcing, inverse, landed, values_landed, cols,
    raw, blocks_in, even_src, odd_src, part, weighed, packed, ends, everyone, values,
    raw_sem, in_sem, w_sem, z_send, z_recv, p_send, p_recv, u_send, u_recv, f_send, f_recv,
):
    fields, points, degrees, group, subs, groups = dims
    tiles = degrees // LANES
    half = tiles // 2
    wide = tiles + half
    blocks = points // ROWS
    sub = lax.axis_index("sub")
    me = lax.axis_index("ma")
    row, lane = grid_iotas()
    is_even = (row & 1) == 0
    parity = lax.rem(me, 2)
    pair = me + 1 - 2 * parity

    def other(k):
        return exclusive_or(me, k, groups)

    middle = groups - 4

    def early_mask(i):
        return groups - 2 + i

    def late_mask(j):
        return 2 + (middle // 2) * (1 - lax.rem(j, 2)) + j // 2

    def fetch(k, f):
        return pltpu.make_async_copy(
            inverse.at[0, f, pl.ds(other(k) * group, group)],
            blocks_in.at[k, f],
            in_sem.at[k, f],
        )

    def load(f, h):
        part_q = pl.ds(h * (points // 2), points // 2)
        return pltpu.make_async_copy(forcing.at[f, part_q], raw.at[f, part_q], raw_sem.at[f, h])

    def send(k, f):
        return pltpu.make_async_remote_copy(
            src_ref=packed.at[k, f], dst_ref=landed.at[k, f],
            send_sem=p_send.at[k, f], recv_sem=p_recv.at[k, f],
            device_id=(sub, other(k)), device_id_type=MESH,
        )

    def send_values(k):
        to = pair if k == 0 else other(k)
        return pltpu.make_async_remote_copy(
            src_ref=values, dst_ref=values_landed.at[1 if k == 0 else k],
            send_sem=u_send.at[k // 2], recv_sem=u_recv.at[k // 2],
            device_id=(sub, to), device_id_type=MESH,
        )

    def forward(k):
        return pltpu.make_async_remote_copy(
            src_ref=values_landed.at[k], dst_ref=values_landed.at[k + 1],
            send_sem=f_send.at[k // 2], recv_sem=f_recv.at[k // 2],
            device_id=(sub, pair), device_id_type=MESH,
        )

    load(0, 0).start()
    load(0, 1).start()
    fetch(early_mask(0), 0).start()
    barrier = pltpu.get_barrier_semaphore()
    subs_to = [lax.rem(sub + n, subs) for n in range(1, subs)]
    for to in subs_to:
        pl.semaphore_signal(barrier, inc=1, device_id=(to, me), device_id_type=MESH)
    for k in range(1, groups):
        pl.semaphore_signal(barrier, inc=1, device_id=(sub, other(k)), device_id_type=MESH)

    m = jnp.zeros((ROWS, LANES), jnp.int32)
    for j in range(ROWS // 2):
        m = jnp.where((row >> 1) == j, slot[2 * j], m)

    def prepare(f, h):
        def one(q, _):
            inside = jnp.where((q > 0) & (q < points - 1), 1.0, 0.0).astype(F32)
            for t in range(tiles):
                at = pl.ds(t * LANES, LANES)
                a = raw[f, q, 0, :, at] * inside
                b = raw[f, q, 1, :, at] * inside
                degree = lane + t * LANES
                mixed = jnp.where(is_even, a, pltpu.roll(b, 1, 0))
                even_src[f, q, t] = jnp.where(degree >= m, mixed, 0.0)
                if t >= half:
                    mixed = jnp.where(is_even, pltpu.roll(a, ROWS - 1, 0), b)
                    odd_src[f, q, t - half] = jnp.where(degree >= degrees - 1 - m, mixed, 0.0)
            return 0

        def two(n, _):
            one(2 * n, 0)
            return one(2 * n + 1, 0)

        lax.fori_loop(h * (points // 4), (h + 1) * (points // 4), two, 0)

    def solve_half(k, f, dest):
        left = jnp.where(lane == MARK, m.astype(F32), 0.0)
        for t in range(tiles):
            at = pl.ds(t * LANES, LANES)
            both = t >= half

            def step(n, sums, t=t, at=at, both=both):
                sums = list(sums)
                for b in range(2):
                    block = 2 * n + b
                    for r in range(ROWS):
                        q = block * ROWS + r
                        even = even_src[f, q, t]
                        odd = odd_src[f, q, t - half] if both else None
                        for p in range(group):
                            line = blocks_in[k, f, p, block, pl.ds(r, 1), at]
                            entry = jnp.broadcast_to(line, (ROWS, LANES))
                            sums[p] += entry * even
                            if both:
                                sums[group + p] += entry * odd
                return tuple(sums)

            count = group * (2 if both else 1)
            start = tuple(jnp.zeros((ROWS, LANES), F32) for _ in range(count))
            sums = lax.fori_loop(0, blocks // 2, step, start)
            for p in range(group):
                part[p, t] = sums[p]
                if both:
                    part[p, tiles + t - half] = sums[group + p]
        for p in range(group):
            pieces, spare = pack([part[p, t] for t in range(wide)], m, degrees)
            for t in range(tiles):
                dest[p * tiles + t] = pieces[t]
            left = jnp.where(lane == p, spare, left)
        dest[group * tiles] = left

    load(0, 0).wait()
    first = early_mask(0)
    load(1, 0).start()
    load(1, 1).start()
    fetch(first, 1).start()
    prepare(0, 0)
    load(0, 1).wait()
    fetch(early_mask(1), 0).start()
    fetch(early_mask(1), 1).start()
    prepare(0, 1)
    fetch(first, 0).wait()
    solve_half(first, 0, packed.at[first, 0])
    pl.semaphore_wait(barrier, subs + groups - 2)
    send(first, 0).start()
    load(1, 0).wait()
    load(1, 1).wait()
    for j in range(middle):
        for f in range(fields):
            fetch(late_mask(j), f).start()
    for k in (1, 0):
        for f in range(fields):
            fetch(k, f).start()
    for h in range(2):
        prepare(1, h)

    def early(h, _):
        k, f = early_mask(h // 2), lax.rem(h, 2)
        fetch(k, f).wait()
        solve_half(k, f, packed.at[k, f])
        send(k, f).start()
        return 0

    lax.fori_loop(1, 2 * fields, early, 0)

    def arrive(j, _):
        for f in range(fields):
            fetch(j, f).wait()
        return 0

    lax.fori_loop(0, groups - 2, arrive, 0)

    mine = blocks // 2
    own_blocks = parity * mine

    def weigh(f, _):
        def add(k, sums):
            sums = list(sums)
            for p in range(group):
                low = edge[0, 0, other(k) * group + p]
                top = edge[0, 1, other(k) * group + p]
                for b in range(mine):
                    for t in range(tiles):
                        entry = blocks_in[k, f, p, own_blocks + b, :, pl.ds(t * LANES, LANES)]
                        n = b * tiles + t
                        sums[n] += low * entry
                        sums[mine * tiles + n] += top * entry
            return tuple(sums)

        start = tuple(jnp.zeros((ROWS, LANES), F32) for _ in range(2 * mine * tiles))
        sums = lax.fori_loop(0, groups, add, start)
        for e in range(2):
            for b in range(mine):
                for t in range(tiles):
                    weighed[own_blocks + b, e, f, t] = sums[(e * mine + b) * tiles + t]
        return 0

    lax.fori_loop(0, fields, weigh, 0)
    shared = weighed.at[pl.ds(own_blocks, mine)]
    swap = pltpu.make_async_remote_copy(
        src_ref=shared, dst_ref=shared, send_sem=w_sem.at[0], recv_sem=w_sem.at[1],
        device_id=(sub, pair), device_id_type=MESH,
    )
    swap.start()

    def late(h, _):
        j, f = h // 2, lax.rem(h, 2)
        k = late_mask(j)
        solve_half(k, f, packed.at[k, f])

        @pl.when((f == 0) | (j < middle - 2))
        def _():
            send(k, f).start()

        return 0

    lax.fori_loop(0, 1, late, 0)
    swap.wait()

    slope_tiles = fields * tiles
    lefts = [jnp.zeros((ROWS, LANES), F32) for _ in range(2)]
    for f in range(fields):
        def slope_step(block, sums, f=f):
            sums = list(sums)
            for r in range(ROWS):
                q = block * ROWS + r
                for t in range(tiles):
                    even = even_src[f, q, t]
                    odd = odd_src[f, q, t - half] if t >= half else None
                    for e in range(2):
                        line = weighed[block, e, f, t, pl.ds(r, 1), :]
                        entry = jnp.broadcast_to(line, (ROWS, LANES))
                        sums[e * wide + t] += entry * even
                        if t >= half:
                            sums[e * wide + t + half] += entry * odd
            return tuple(sums)

        start = tuple(jnp.zeros((ROWS, LANES), F32) for _ in range(2 * wide))
        sums = lax.fori_loop(0, blocks, slope_step, start)
        for e in range(2):
            pieces, spare = pack(list(sums[e * wide:(e + 1) * wide]), m, degrees)
            for t in range(tiles):
                ends[e, f * tiles + t] = pieces[t]
            lefts[e] = jnp.where(lane == f, spare, lefts[e])
            for w in range(2):
                for t in range(tiles):
                    line = weighed[w * (blocks - 1), e, f, t, pl.ds(w * (ROWS - 1), 1), :]
                    ends[e, slope_tiles + 1 + t, pl.ds(f * 2 + w, 1), :] = line
    for e in range(2):
        ends[e, slope_tiles] = lefts[e]

    def holds(s, e):
        return s > 0 if e == 0 else s < subs - 1

    def exchange(n, e):
        return pltpu.make_async_remote_copy(
            src_ref=ends.at[e], dst_ref=everyone.at[sub, e],
            send_sem=z_send.at[n, e], recv_sem=z_recv.at[n, e],
            device_id=(subs_to[n], me), device_id_type=MESH,
        )

    for n in range(subs - 1):
        for e in range(2):
            @pl.when(holds(sub, e))
            def _(n=n, e=e):
                exchange(n, e).start()

    everyone[sub] = ends[...]

    lax.fori_loop(1, middle * fields, late, 0)

    def to_pair(f, _):
        solve_half(1, f, packed.at[1, f])
        send(1, f).start()
        return 0

    lax.fori_loop(0, fields, to_pair, 0)

    def to_self(f, _):
        solve_half(0, f, landed.at[0, f])
        return 0

    lax.fori_loop(0, fields, to_self, 0)
    for f in range(fields):
        for p in range(group):
            cols[0, f, pl.ds(p, 1), :] = blocks_in[0, f, p, 0, pl.ds(0, 1), :]
            cols[1, f, pl.ds(p, 1), :] = blocks_in[0, f, p, blocks - 1, pl.ds(ROWS - 1, 1), :]

    for n in range(subs - 1):
        sender = lax.rem(sub + subs - n - 1, subs)
        for e in range(2):
            @pl.when(holds(sub, e))
            def _(n=n, e=e):
                exchange(n, e).wait_send()

            @pl.when(holds(sender, e))
            def _(n=n, e=e):
                exchange(n, e).wait_recv()

    spares = jnp.zeros((ROWS, LANES), F32)
    for f in range(fields):
        def slopes(s, e):
            pieces = [everyone[s, e, f * tiles + t] for t in range(tiles)]
            return unpack(pieces, spread(everyone[s, e, slope_tiles], f), m, degrees)

        rights = []
        for k in range(subs - 1):
            low, top = slopes(k + 1, 0), slopes(k, 1)
            rights.append([low[t] - top[t] for t in range(wide)])
        lower, upper = [], []
        for t in range(wide):
            source = t if t < tiles else t - half

            def influence(s, e, w):
                line = everyone[s, e, slope_tiles + 1 + source, pl.ds(f * 2 + w, 1), :]
                return jnp.broadcast_to(line, (ROWS, LANES))

            zero = jnp.zeros((ROWS, LANES), F32)
            ratio, reduced = zero, zero
            ratios, reduceds = [], []
            for k in range(subs - 1):
                low = influence(k, 1, 0)
                diagonal = influence(k, 1, 1) - influence(k + 1, 0, 0)
                up = -influence(k + 1, 0, 1)
                pivot = diagonal - low * ratio
                reduced = (rights[k][t] - low * reduced) / pivot
                ratio = up / pivot
                ratios.append(ratio)
                reduceds.append(reduced)
            later = zero
            lower_value, upper_value = zero, zero
            for k in range(subs - 2, -1, -1):
                later = reduceds[k] - ratios[k] * later
                lower_value = jnp.where(sub == k + 1, later, lower_value)
                upper_value = jnp.where(sub == k, later, upper_value)
            lower.append(lower_value)
            upper.append(upper_value)
        for e, vector in enumerate((lower, upper)):
            pieces, spare = pack(vector, m, degrees)
            for t in range(tiles):
                values[(e * fields + f) * tiles + t] = pieces[t]
            spares = jnp.where(lane == e * fields + f, spare, spares)
    values[2 * fields * tiles] = spares

    masks = list(range(groups - 2, 0, -2))
    for k in masks + [0]:
        send_values(k).start()
    for j in range(middle - 2, middle):
        send(late_mask(j), 1).start()
    values_landed[0] = values[...]
    for k in masks:
        send_values(k).wait_recv()
        forward(k).start()
    for k in range(1, groups):
        for f in range(fields):
            send(k, f).wait()
    send_values(0).wait()
    for k in masks:
        send_values(k).wait_send()
        forward(k).wait()


def finish_kernel(dims, landed, values, cols, result, out, out_sem):
    fields, degrees, group, groups = dims
    tiles = degrees // LANES
    half = tiles // 2
    wide = tiles + half
    me = lax.axis_index("ma")
    row, lane = grid_iotas()
    is_even = (row & 1) == 0

    def put(k):
        at = exclusive_or(me, k, groups) * ROWS
        rows = pl.ds(pl.multiple_of(at, ROWS), ROWS)
        return pltpu.make_async_copy(out.at[k], result.at[:, :, :, rows, :], out_sem.at[k])

    def one(k, _):
        for f in range(fields):
            left = landed[k, f, group * tiles]
            m = spread(left, MARK).astype(jnp.int32)
            added = []
            for e in range(2):
                n = e * fields + f
                pieces = [values[k, n * tiles + t] for t in range(tiles)]
                spare = spread(values[k, 2 * fields * tiles], n)
                added.append(unpack(pieces, spare, m, degrees))
            for p in range(group):
                pieces = [landed[k, f, p * tiles + t] for t in range(tiles)]
                full = unpack(pieces, spread(left, p), m, degrees)
                for t in range(tiles):
                    at = pl.ds(t * LANES, LANES)
                    low = jnp.broadcast_to(cols[0, f, pl.ds(p, 1), at], (ROWS, LANES))
                    top = jnp.broadcast_to(cols[1, f, pl.ds(p, 1), at], (ROWS, LANES))
                    e = full[t] + added[0][t] * low
                    e = e + added[1][t] * top
                    o = jnp.zeros((ROWS, LANES), F32)
                    if t >= half:
                        spot = tiles + t - half
                        o = full[spot] + added[0][spot] * low
                        o = o + added[1][spot] * top
                    out[k, f, p, 0, :, at] = jnp.where(is_even, e, pltpu.roll(o, 1, 0))
                    out[k, f, p, 1, :, at] = jnp.where(is_even, pltpu.roll(e, ROWS - 1, 0), o)
        put(k).start()
        return 0

    lax.fori_loop(0, groups, one, 0)
    for k in range(groups):
        put(k).wait()


def in_hbm(x):
    return pltpu.with_memory_space_constraint(x, pltpu.HBM)


def body(forcing, slot_wavenumber, inverse, edge_weights):
    fields, points, halves, slots, degrees = forcing.shape
    subs, groups = lax.axis_size("sub"), lax.axis_size("ma")
    group = points // groups
    tiles = degrees // LANES
    half = tiles // 2
    wide = tiles + half
    assert halves == 2 and slots == ROWS and tiles == 4 and fields == 2
    assert groups >= 8 and groups & (groups - 1) == 0 and group < MARK
    count = group * tiles + 1
    end_count = fields * tiles + 1 + tiles
    value_count = 2 * fields * tiles + 1
    shape = jax.ShapeDtypeStruct
    blocks = points // ROWS
    dma = pltpu.SemaphoreType.DMA
    landed, values, cols = pl.pallas_call(
        functools.partial(solve_kernel, (fields, points, degrees, group, subs, groups)),
        in_specs=[
            pl.BlockSpec(memory_space=pltpu.SMEM),
            pl.BlockSpec(memory_space=pltpu.SMEM),
            pl.BlockSpec(memory_space=pltpu.HBM),
            pl.BlockSpec(memory_space=pltpu.HBM),
        ],
        out_specs=[
            pl.BlockSpec(memory_space=pltpu.VMEM),
            pl.BlockSpec(memory_space=pltpu.VMEM),
            pl.BlockSpec(memory_space=pltpu.VMEM),
        ],
        out_shape=[
            shape((groups, fields, count, ROWS, LANES), F32),
            shape((groups, value_count, ROWS, LANES), F32),
            shape((2, fields, group, degrees), F32),
        ],
        scratch_shapes=[
            pltpu.VMEM((fields, points, halves, slots, degrees), F32),
            pltpu.VMEM((groups, fields, group, blocks, ROWS, degrees), F32),
            pltpu.VMEM((fields, points, tiles, ROWS, LANES), F32),
            pltpu.VMEM((fields, points, half, ROWS, LANES), F32),
            pltpu.VMEM((group, wide, ROWS, LANES), F32),
            pltpu.VMEM((blocks, 2, fields, tiles, ROWS, LANES), F32),
            pltpu.VMEM((groups, fields, count, ROWS, LANES), F32),
            pltpu.VMEM((2, end_count, ROWS, LANES), F32),
            pltpu.VMEM((subs, 2, end_count, ROWS, LANES), F32),
            pltpu.VMEM((value_count, ROWS, LANES), F32),
            dma((fields, 2)),
            dma((groups, fields)),
            dma((2,)),
            dma((subs - 1, 2)),
            dma((subs - 1, 2)),
            dma((groups, fields)),
            dma((groups, fields)),
            dma((groups // 2,)),
            dma((groups // 2,)),
            dma((groups // 2,)),
            dma((groups // 2,)),
        ],
        compiler_params=pltpu.CompilerParams(
            collective_id=0, has_side_effects=True, vmem_limit_bytes=VMEM_BYTES
        ),
    )(
        in_hbm(slot_wavenumber),
        in_hbm(edge_weights),
        in_hbm(forcing),
        in_hbm(inverse.reshape(1, fields, points, blocks, ROWS, degrees)),
    )

    return pl.pallas_call(
        functools.partial(finish_kernel, (fields, degrees, group, groups)),
        in_specs=[
            pl.BlockSpec(memory_space=pltpu.VMEM),
            pl.BlockSpec(memory_space=pltpu.VMEM),
            pl.BlockSpec(memory_space=pltpu.VMEM),
        ],
        out_specs=pl.BlockSpec(memory_space=pl.ANY),
        out_shape=shape((fields, group, halves, slots * groups, degrees), F32),
        scratch_shapes=[
            pltpu.VMEM((groups, fields, group, halves, slots, degrees), F32),
            dma((groups,)),
        ],
        compiler_params=pltpu.CompilerParams(vmem_limit_bytes=16 * 1024 * 1024),
    )(landed, values, cols)


def solution(mesh):
    return jax.shard_map(
        body,
        mesh=mesh,
        in_specs=(
            P(None, "sub", None, "ma", None),
            P("ma"),
            P("sub", None, None, None, None),
            P("sub", None, None),
        ),
        out_specs=P(None, ("sub", "ma"), None, None, None),
        check_vma=False,
    )
```

time: 49.7 us -> 38.3 us (0.77)
  the two profiles are of different devices: /device:TPU:3 before, /device:TPU:0 now
where the time goes in v1:
time: 38.3 us; the launch traced here: 38.2 us
  Pallas kernels  38.2 us (100%)
    pallas_call x1, Pallas kernels, body(): pl.pallas_call(functools.partial(solve_kernel, (fields, points, degrees,...  35.5 us
    pallas_call x1, Pallas kernels, body(): pl.pallas_call(functools.partial(finish_kernel, (fields, degrees, group,...  2.69 us

profile of v1, /device:TPU:0, one launch (start us, length us, event | category | flops | bytes accessed | tf_op | source)
XLA Modules:
  0.0 38.2 jit_solution(18287986657336929855)
XLA Ops:
  0.0 35.5 %shard_map.46 = (f32[8,2,33,8,128]{4,3,2,1,0:T(8,128)S(1)}, f32[8,17,8,128]{3,2,1,0:T(8,128)S(1)}, f32[2,2,8,512]{3,2,1,0:T(8,128)S(1)}) custom-call(s32[8]{0:T(128)} %slot.1, f32[1,2,64]{2,1,0:T(2,128)} %edge.1, f32[2,64,2,8,512]{4,3,2,1,0:T(8,128)} %forcing.1, f32[1,2,64,8,8,512]{5,4,3,2,1,0:T(8,128)} %bitcast.1), custom_call_target="tpu_custom_call" | custom-call | tf_op jit(solution)/shard_map/pallas_call | solution.py:511
  35.5 2.7 %shard_map.47 = f32[2,8,2,64,512]{4,3,2,1,0:T(8,128)} custom-call(f32[8,2,33,8,128]{4,3,2,1,0:T(8,128)S(1)} %get-tuple-element.8.landed, f32[8,17,8,128]{3,2,1,0:T(8,128)S(1)} %get-tuple-element.9.values, f32[2,2,8,512]{3,2,1,0:T(8,128)S(1)} %get-tuple-element.10.cols), custom_call_target="tpu_custom_call" | custom-call | tf_op jit(solution)/shard_map/pallas_call | solution.py:562

commit v2 on v1

v2 whole, which is shorter than its diff:
```python
import functools

import jax
import jax.numpy as jnp
from jax import lax
from jax.experimental import pallas as pl
from jax.experimental.pallas import tpu as pltpu
from jax.sharding import PartitionSpec as P

LANES = 128
ROWS = 8
F32 = jnp.float32
MESH = pl.DeviceIdType.MESH
MARK = 64
VMEM_BYTES = 40 * 1024 * 1024


def grid_iotas():
    row = lax.broadcasted_iota(jnp.int32, (ROWS, LANES), 0)
    lane = lax.broadcasted_iota(jnp.int32, (ROWS, LANES), 1)
    return row, lane


def lane_gather(values, index):
    return jnp.take_along_axis(values, index, axis=1, mode="promise_in_bounds")


def spread(values, k):
    return lane_gather(values, jnp.full((ROWS, LANES), k, jnp.int32))


def exclusive_or(a, b, groups):
    total = 0
    bit = 1
    while bit < groups:
        total = total + lax.rem(a // bit + b // bit, 2) * bit
        bit *= 2
    return total


def pack(pieces, m, degrees):
    _, lane = grid_iotas()
    shift_index = (lane - m) & (LANES - 1)
    left_index = (degrees - 1 - m) & (LANES - 1)
    near, far = pieces[4], pieces[5]
    near_moved = lane_gather(near, shift_index)
    far_moved = lane_gather(far, shift_index)
    first = jnp.where(
        lane >= m, pieces[0], jnp.where(lane - m >= -LANES, far_moved, near_moved)
    )
    second = jnp.where(lane + LANES >= m, pieces[1], far_moved)
    spare = jnp.where(m < LANES, lane_gather(far, left_index), lane_gather(near, left_index))
    return [first, second, pieces[2], pieces[3]], spare


def unpack(pieces, spare, m, degrees):
    _, lane = grid_iotas()
    back_index = (lane + m) & (LANES - 1)
    first = lane_gather(pieces[0], back_index)
    second = lane_gather(pieces[1], back_index)
    moved = [first, jnp.where(lane + m < 2 * LANES, first, second)]
    odd = []
    for t in range(2):
        degree = lane + (2 + t) * LANES
        odd.append(
            jnp.where(
                degree >= degrees - m,
                moved[t],
                jnp.where(degree == degrees - 1 - m, spare, 0.0),
            )
        )
    even = [
        jnp.where(lane >= m, pieces[0], 0.0),
        jnp.where(lane + LANES >= m, pieces[1], 0.0),
        pieces[2],
        pieces[3],
    ]
    return even + odd


def solve_kernel(
    dims, slot_in, edge_in, forcing, inverse, landed, values_landed, cols,
    slot, edge, raw, blocks_in, even_src, odd_src, part, stash, weighed, packed, ends, everyone,
    uvals, values,
    small_sem, raw_sem, in_sem, w_sem, z_send, z_recv, p_sem, u_sem, f_sem,
):
    fields, points, degrees, group, subs, groups = dims
    tiles = degrees // LANES
    half = tiles // 2
    wide = tiles + half
    blocks = points // ROWS
    sub = lax.axis_index("sub")
    me = lax.axis_index("ma")
    row, lane = grid_iotas()
    is_even = (row & 1) == 0
    parity = lax.rem(me, 2)
    pair = me + 1 - 2 * parity
    far = groups - 2
    middle = groups - 4
    spot_left, spot_influence = tiles, tiles + 1

    def other(k):
        return exclusive_or(me, k, groups)

    def late_mask(j):
        return 2 + (middle // 2) * (1 - lax.rem(j, 2)) + j // 2

    def fetch(k, f):
        index = 0
        if isinstance(k, int) and k >= far:
            index = k - far + 1
        return pltpu.make_async_copy(
            inverse.at[0, f, pl.ds(other(k) * group, group)],
            blocks_in.at[k, f],
            in_sem.at[index, f],
        )

    def rest_arrives(f):
        most = blocks_in.at[pl.ds(0, far), f]
        pltpu.make_async_copy(most, most, in_sem.at[0, f]).wait()

    def load(f, h):
        part_q = pl.ds(h * (points // 2), points // 2)
        return pltpu.make_async_copy(forcing.at[f, part_q], raw.at[f, part_q], raw_sem.at[f, h])

    def send(k, f):
        return pltpu.make_async_remote_copy(
            src_ref=packed.at[k, f], dst_ref=landed.at[k, f],
            send_sem=p_sem.at[0], recv_sem=p_sem.at[1],
            device_id=(sub, other(k)), device_id_type=MESH,
        )

    def send_values(f):
        return pltpu.make_async_remote_copy(
            src_ref=values.at[f], dst_ref=values_landed.at[0, f],
            send_sem=u_sem.at[0, f], recv_sem=u_sem.at[1, f],
            device_id=(sub, other(far)), device_id_type=MESH,
        )

    def forward(f):
        return pltpu.make_async_remote_copy(
            src_ref=values_landed.at[0, f], dst_ref=values_landed.at[1, f],
            send_sem=f_sem.at[0, f], recv_sem=f_sem.at[1, f],
            device_id=(sub, pair), device_id_type=MESH,
        )

    load(0, 0).start()
    load(0, 1).start()
    fetch(far, 0).start()
    slot_copy = pltpu.make_async_copy(slot_in, slot, small_sem.at[0])
    edge_copy = pltpu.make_async_copy(edge_in, edge, small_sem.at[1])
    slot_copy.start()
    edge_copy.start()
    barrier = pltpu.get_barrier_semaphore()
    subs_to = [lax.rem(sub + n, subs) for n in range(1, subs)]
    for to in subs_to:
        pl.semaphore_signal(barrier, inc=1, device_id=(to, me), device_id_type=MESH)
    for k in range(1, groups):
        pl.semaphore_signal(barrier, inc=1, device_id=(sub, other(k)), device_id_type=MESH)
    fetch(far + 1, 0).start()
    slot_copy.wait()
    edge_copy.wait()

    m = jnp.zeros((ROWS, LANES), jnp.int32)
    for j in range(ROWS // 2):
        m = jnp.where((row >> 1) == j, slot[2 * j], m)

    def prepare(f, h):
        def one(q):
            inside = jnp.where((q > 0) & (q < points - 1), 1.0, 0.0).astype(F32)
            for t in range(tiles):
                at = pl.ds(t * LANES, LANES)
                a = raw[f, q, 0, :, at] * inside
                b = raw[f, q, 1, :, at] * inside
                degree = lane + t * LANES
                mixed = jnp.where(is_even, a, pltpu.roll(b, 1, 0))
                even_src[f, q, t] = jnp.where(degree >= m, mixed, 0.0)
                if t >= half:
                    mixed = jnp.where(is_even, pltpu.roll(a, ROWS - 1, 0), b)
                    odd_src[f, q, t - half] = jnp.where(degree >= degrees - 1 - m, mixed, 0.0)

        def two(n, _):
            one(2 * n)
            one(2 * n + 1)
            return 0

        lax.fori_loop(h * (points // 4), (h + 1) * (points // 4), two, 0)

    def solve_half(k, f, into):
        for t in range(tiles):
            at = pl.ds(t * LANES, LANES)
            both = t >= half

            def step(n, sums, t=t, at=at, both=both):
                sums = list(sums)
                for b in range(2):
                    block = 2 * n + b
                    for r in range(ROWS):
                        q = block * ROWS + r
                        even = even_src[f, q, t]
                        odd = odd_src[f, q, t - half] if both else None
                        for p in range(group):
                            line = blocks_in[k, f, p, block, pl.ds(r, 1), at]
                            entry = jnp.broadcast_to(line, (ROWS, LANES))
                            sums[p] += entry * even
                            if both:
                                sums[group + p] += entry * odd
                return tuple(sums)

            count = group * (2 if both else 1)
            start = tuple(jnp.zeros((ROWS, LANES), F32) for _ in range(count))
            sums = lax.fori_loop(0, blocks // 2, step, start)
            for p in range(group):
                into[p, t] = sums[p]
                if both:
                    into[p, tiles + t - half] = sums[group + p]

    def write_half(k, f, source, dest, fold):
        left = jnp.where(lane == MARK, m.astype(F32), 0.0)
        for p in range(group):
            full = [source[p, t] for t in range(wide)]
            if fold:
                for t in range(tiles):
                    at = pl.ds(t * LANES, LANES)
                    line = blocks_in[k, f, p, 0, pl.ds(0, 1), at]
                    low = jnp.broadcast_to(line, (ROWS, LANES))
                    line = blocks_in[k, f, p, blocks - 1, pl.ds(ROWS - 1, 1), at]
                    top = jnp.broadcast_to(line, (ROWS, LANES))
                    for n in (t,) if t < half else (t, t + half):
                        full[n] = full[n] + uvals[f, 0, n] * low
                        full[n] = full[n] + uvals[f, 1, n] * top
            pieces, spare = pack(full, m, degrees)
            for t in range(tiles):
                dest[p * tiles + t] = pieces[t]
            left = jnp.where(lane == p, spare, left)
        dest[group * tiles] = left

    def early(k, f):
        fetch(k, f).wait()
        solve_half(k, f, part)
        write_half(k, f, part, packed.at[k, f], False)

    mine = blocks // 2
    own_blocks = parity * mine

    def weigh(f):
        def add(k, sums):
            sums = list(sums)
            for p in range(group):
                low = edge[0, 0, other(k) * group + p]
                top = edge[0, 1, other(k) * group + p]
                for b in range(mine):
                    for t in range(tiles):
                        entry = blocks_in[k, f, p, own_blocks + b, :, pl.ds(t * LANES, LANES)]
                        n = b * tiles + t
                        sums[n] += low * entry
                        sums[mine * tiles + n] += top * entry
            return tuple(sums)

        start = tuple(jnp.zeros((ROWS, LANES), F32) for _ in range(2 * mine * tiles))
        sums = lax.fori_loop(0, groups, add, start)
        for e in range(2):
            for b in range(mine):
                for t in range(tiles):
                    weighed[f, own_blocks + b, e, t] = sums[(e * mine + b) * tiles + t]

    def swap(f):
        shared = weighed.at[f, pl.ds(own_blocks, mine)]
        return pltpu.make_async_remote_copy(
            src_ref=shared, dst_ref=shared, send_sem=w_sem.at[0, f], recv_sem=w_sem.at[1, f],
            device_id=(sub, pair), device_id_type=MESH,
        )

    def exchange(n, f, sender, begin):
        outer = (sender == 0) | (sender == subs - 1)
        first = 1 - lax.min(sender, 1)
        for count, case in ((1, outer), (2, jnp.logical_not(outer))):
            kept = pl.ds(first, count) if count == 1 else pl.ds(0, 2)
            copy = pltpu.make_async_remote_copy(
                src_ref=ends.at[f, kept], dst_ref=everyone.at[sender, f, kept],
                send_sem=z_send.at[n, f], recv_sem=z_recv.at[n, f],
                device_id=(subs_to[n], me), device_id_type=MESH,
            )

            @pl.when(case)
            def _(copy=copy):
                begin(copy)

    def slopes(f):
        def slope_step(block, sums):
            sums = list(sums)
            for r in range(ROWS):
                q = block * ROWS + r
                for t in range(tiles):
                    even = even_src[f, q, t]
                    odd = odd_src[f, q, t - half] if t >= half else None
                    for e in range(2):
                        line = weighed[f, block, e, t, pl.ds(r, 1), :]
                        entry = jnp.broadcast_to(line, (ROWS, LANES))
                        sums[e * wide + t] += entry * even
                        if t >= half:
                            sums[e * wide + t + half] += entry * odd
            return tuple(sums)

        start = tuple(jnp.zeros((ROWS, LANES), F32) for _ in range(2 * wide))
        sums = lax.fori_loop(0, blocks, slope_step, start)
        for e in range(2):
            pieces, spare = pack(list(sums[e * wide:(e + 1) * wide]), m, degrees)
            for t in range(tiles):
                ends[f, e, t] = pieces[t]
            ends[f, e, spot_left] = spare
            for w in range(2):
                for t in range(tiles):
                    line = weighed[f, w * (blocks - 1), e, t, pl.ds(w * (ROWS - 1), 1), :]
                    ends[f, e, spot_influence, pl.ds(2 * t + w, 1), :] = line
        for n in range(subs - 1):
            exchange(n, f, sub, lambda copy: copy.start())
        everyone[sub, f] = ends[f]

    def interface(f):
        for n in range(subs - 1):
            exchange(n, f, sub, lambda copy: copy.wait_send())
            sender = lax.rem(sub + subs - n - 1, subs)
            exchange(n, f, sender, lambda copy: copy.wait_recv())

        def slopes_of(s, e):
            pieces = [everyone[s, f, e, t] for t in range(tiles)]
            return unpack(pieces, everyone[s, f, e, spot_left], m, degrees)

        rights = []
        for k in range(subs - 1):
            low, top = slopes_of(k + 1, 0), slopes_of(k, 1)
            rights.append([low[t] - top[t] for t in range(wide)])
        lower, upper = [], []
        for t in range(wide):
            source = t if t < tiles else t - half

            def influence(s, e, w):
                line = everyone[s, f, e, spot_influence, pl.ds(2 * source + w, 1), :]
                return jnp.broadcast_to(line, (ROWS, LANES))

            zero = jnp.zeros((ROWS, LANES), F32)
            ratio, reduced = zero, zero
            ratios, reduceds = [], []
            for k in range(subs - 1):
                low = influence(k, 1, 0)
                diagonal = influence(k, 1, 1) - influence(k + 1, 0, 0)
                up = -influence(k + 1, 0, 1)
                pivot = diagonal - low * ratio
                reduced = (rights[k][t] - low * reduced) / pivot
                ratio = up / pivot
                ratios.append(ratio)
                reduceds.append(reduced)
            later = zero
            lower_value, upper_value = zero, zero
            for k in range(subs - 2, -1, -1):
                later = reduceds[k] - ratios[k] * later
                lower_value = jnp.where(sub == k + 1, later, lower_value)
                upper_value = jnp.where(sub == k, later, upper_value)
            lower.append(lower_value)
            upper.append(upper_value)
        spares = jnp.zeros((ROWS, LANES), F32)
        for e, vector in enumerate((lower, upper)):
            for t in range(wide):
                uvals[f, e, t] = vector[t]
            pieces, spare = pack(vector, m, degrees)
            for t in range(tiles):
                values[f, e * tiles + t] = pieces[t]
            spares = jnp.where(lane == e, spare, spares)
        values[f, 2 * tiles] = spares
        send_values(f).start()

    def late_parts(j, f):
        solve_half(late_mask(j), f, stash.at[j])

    def late_write(f):
        def one(j, _):
            k = late_mask(j)
            write_half(k, f, stash.at[j], packed.at[k, f], True)
            send(k, f).start()
            return 0

        lax.fori_loop(0, middle, one, 0)

    load(0, 0).wait()
    load(1, 0).start()
    load(1, 1).start()
    prepare(0, 0)
    load(0, 1).wait()
    for k in range(far):
        fetch(k, 0).start()
    prepare(0, 1)
    early(far, 0)
    for k in (far, far + 1):
        fetch(k, 1).start()
    pl.semaphore_wait(barrier, subs + groups - 2)
    send(far, 0).start()
    for k in range(far):
        fetch(k, 1).start()
    early(far + 1, 0)
    send(far + 1, 0).start()
    rest_arrives(0)
    weigh(0)
    swap(0).start()
    for h in range(2):
        load(1, h).wait()
        prepare(1, h)
    early(far, 1)
    send(far, 1).start()
    swap(0).wait()
    slopes(0)
    early(far + 1, 1)
    send(far + 1, 1).start()
    rest_arrives(1)
    weigh(1)
    swap(1).start()
    late_parts(0, 0)
    swap(1).wait()
    slopes(1)

    def more(f):
        def one(j, _):
            late_parts(j, f)
            return 0

        lax.fori_loop(1 - f, middle, one, 0)

    def turn(f, _):
        more(f)
        interface(f)
        late_write(f)
        return 0

    lax.fori_loop(0, fields, turn, 0)

    def to_pair(f, _):
        solve_half(1, f, part)
        write_half(1, f, part, packed.at[1, f], True)
        send(1, f).start()
        return 0

    lax.fori_loop(0, fields, to_pair, 0)
    for f in range(fields):
        send_values(f).wait_recv()
        forward(f).start()

    def to_self(f, _):
        solve_half(0, f, part)
        write_half(0, f, part, landed.at[0, f], True)
        return 0

    lax.fori_loop(0, fields, to_self, 0)
    for f in range(fields):
        for p in range(group):
            cols[0, f, pl.ds(p, 1), :] = blocks_in[0, f, p, 0, pl.ds(0, 1), :]
            cols[1, f, pl.ds(p, 1), :] = blocks_in[0, f, p, blocks - 1, pl.ds(ROWS - 1, 1), :]
    for f in range(fields):
        send_values(f).wait_send()
        forward(f).wait()
    away = pl.ds(1, groups - 1)
    pltpu.make_async_remote_copy(
        src_ref=packed.at[away], dst_ref=landed.at[away],
        send_sem=p_sem.at[0], recv_sem=p_sem.at[1],
        device_id=(sub, pair), device_id_type=MESH,
    ).wait()


def finish_kernel(dims, landed, values, cols, result, out, out_sem):
    fields, degrees, group, groups = dims
    tiles = degrees // LANES
    half = tiles // 2
    me = lax.axis_index("ma")
    row, _ = grid_iotas()
    is_even = (row & 1) == 0
    far = groups - 2

    def put(k):
        at = exclusive_or(me, k, groups) * ROWS
        rows = pl.ds(pl.multiple_of(at, ROWS), ROWS)
        return pltpu.make_async_copy(out.at[k], result.at[:, :, :, rows, :], out_sem.at[k])

    def one(k, fold):
        for f in range(fields):
            left = landed[k, f, group * tiles]
            m = spread(left, MARK).astype(jnp.int32)
            added = []
            for e in range(2 if fold else 0):
                pieces = [values[k - far, f, e * tiles + t] for t in range(tiles)]
                spare = spread(values[k - far, f, 2 * tiles], e)
                added.append(unpack(pieces, spare, m, degrees))
            for p in range(group):
                pieces = [landed[k, f, p * tiles + t] for t in range(tiles)]
                full = unpack(pieces, spread(left, p), m, degrees)
                for t in range(tiles):
                    at = pl.ds(t * LANES, LANES)
                    spots = (t,) if t < half else (t, t + half)
                    if fold:
                        low = jnp.broadcast_to(cols[0, f, pl.ds(p, 1), at], (ROWS, LANES))
                        top = jnp.broadcast_to(cols[1, f, pl.ds(p, 1), at], (ROWS, LANES))
                        for n in spots:
                            full[n] = full[n] + added[0][n] * low
                            full[n] = full[n] + added[1][n] * top
                    e = full[t]
                    o = full[t + half] if t >= half else jnp.zeros((ROWS, LANES), F32)
                    out[k, f, p, 0, :, at] = jnp.where(is_even, e, pltpu.roll(o, 1, 0))
                    out[k, f, p, 1, :, at] = jnp.where(is_even, pltpu.roll(e, ROWS - 1, 0), o)
        put(k).start()

    def plain(k, _):
        one(k, False)
        return 0

    def folded(k, _):
        one(k, True)
        return 0

    lax.fori_loop(0, far, plain, 0)
    lax.fori_loop(far, groups, folded, 0)
    for k in range(groups):
        put(k).wait()


def in_hbm(x):
    return pltpu.with_memory_space_constraint(x, pltpu.HBM)


def body(forcing, slot_wavenumber, inverse, edge_weights):
    fields, points, halves, slots, degrees = forcing.shape
    subs, groups = lax.axis_size("sub"), lax.axis_size("ma")
    group = points // groups
    tiles = degrees // LANES
    half = tiles // 2
    wide = tiles + half
    assert halves == 2 and slots == ROWS and tiles == 4 and fields == 2
    assert groups >= 8 and groups & (groups - 1) == 0 and group < MARK
    count = group * tiles + 1
    end_count = tiles + 2
    value_count = 2 * tiles + 1
    shape = jax.ShapeDtypeStruct
    blocks = points // ROWS
    dma = pltpu.SemaphoreType.DMA
    landed, values, cols = pl.pallas_call(
        functools.partial(solve_kernel, (fields, points, degrees, group, subs, groups)),
        in_specs=[pl.BlockSpec(memory_space=pltpu.HBM)] * 4,
        out_specs=[pl.BlockSpec(memory_space=pltpu.VMEM)] * 3,
        out_shape=[
            shape((groups, fields, count, ROWS, LANES), F32),
            shape((2, fields, value_count, ROWS, LANES), F32),
            shape((2, fields, group, degrees), F32),
        ],
        scratch_shapes=[
            pltpu.SMEM(slot_wavenumber.shape, slot_wavenumber.dtype),
            pltpu.SMEM(edge_weights.shape, F32),
            pltpu.VMEM((fields, points, halves, slots, degrees), F32),
            pltpu.VMEM((groups, fields, group, blocks, ROWS, degrees), F32),
            pltpu.VMEM((fields, points, tiles, ROWS, LANES), F32),
            pltpu.VMEM((fields, points, half, ROWS, LANES), F32),
            pltpu.VMEM((group, wide, ROWS, LANES), F32),
            pltpu.VMEM((groups - 4, group, wide, ROWS, LANES), F32),
            pltpu.VMEM((fields, blocks, 2, tiles, ROWS, LANES), F32),
            pltpu.VMEM((groups, fields, count, ROWS, LANES), F32),
            pltpu.VMEM((fields, 2, end_count, ROWS, LANES), F32),
            pltpu.VMEM((subs, fields, 2, end_count, ROWS, LANES), F32),
            pltpu.VMEM((fields, 2, wide, ROWS, LANES), F32),
            pltpu.VMEM((fields, value_count, ROWS, LANES), F32),
            dma((2,)),
            dma((fields, 2)),
            dma((3, fields)),
            dma((2, fields)),
            dma((subs - 1, fields)),
            dma((subs - 1, fields)),
            dma((2,)),
            dma((2, fields)),
            dma((2, fields)),
        ],
        compiler_params=pltpu.CompilerParams(
            collective_id=0, has_side_effects=True, vmem_limit_bytes=VMEM_BYTES
        ),
    )(
        in_hbm(slot_wavenumber),
        in_hbm(edge_weights),
        in_hbm(forcing),
        in_hbm(inverse.reshape(1, fields, points, blocks, ROWS, degrees)),
    )

    return pl.pallas_call(
        functools.partial(finish_kernel, (fields, degrees, group, groups)),
        in_specs=[
            pl.BlockSpec(memory_space=pltpu.VMEM),
            pl.BlockSpec(memory_space=pltpu.VMEM),
            pl.BlockSpec(memory_space=pltpu.VMEM),
        ],
        out_specs=pl.BlockSpec(memory_space=pl.ANY),
        out_shape=shape((fields, group, halves, slots * groups, degrees), F32),
        scratch_shapes=[
            pltpu.VMEM((groups, fields, group, halves, slots, degrees), F32),
            dma((groups,)),
        ],
        compiler_params=pltpu.CompilerParams(vmem_limit_bytes=16 * 1024 * 1024),
    )(landed, values, cols)


def solution(mesh):
    return jax.shard_map(
        body,
        mesh=mesh,
        in_specs=(
            P(None, "sub", None, "ma", None),
            P("ma"),
            P("sub", None, None, None, None),
            P("sub", None, None),
        ),
        out_specs=P(None, ("sub", "ma"), None, None, None),
        check_vma=False,
    )
```

time: 38.3 us -> 35.7 us (0.932)
  Pallas kernels: 38.2 us -> 35.5 us
    pallas_call x1, Pallas kernels: 35.5 us -> 33 us  [body(): pl.pallas_call(functools.partial(solve_kernel, (fields, points, degrees,...]
where the time goes in v2:
time: 35.7 us; the launch traced here: 35.6 us
  Pallas kernels  35.5 us (99%)
    pallas_call x1, Pallas kernels, body(): pl.pallas_call(functools.partial(solve_kernel, (fields, points, degrees,...  33 us
    pallas_call x1, Pallas kernels, body(): pl.pallas_call(functools.partial(finish_kernel, (fields, degrees, group,...  2.56 us

profile of v2, /device:TPU:0, one launch (start us, length us, event | category | flops | bytes accessed | tf_op | source)
XLA Modules:
  0.0 35.6 jit_solution(9164136060634376655)
XLA Ops:
  0.0 33.0 %shard_map.46 = (f32[8,2,33,8,128]{4,3,2,1,0:T(8,128)S(1)}, f32[2,2,9,8,128]{4,3,2,1,0:T(8,128)S(1)}, f32[2,2,8,512]{3,2,1,0:T(8,128)S(1)}) custom-call(s32[8]{0:T(128)} %slot_in.1, f32[1,2,64]{2,1,0:T(2,128)} %edge_in.1, f32[2,64,2,8,512]{4,3,2,1,0:T(8,128)} %forcing.1, f32[1,2,64,8,8,512]{5,4,3,2,1,0:T(8,128)} %bitcast.1), custom_call_target="tpu_custom_call" | custom-call | tf_op jit(solution)/shard_map/pallas_call | solution.py:542
  33.0 2.6 %shard_map.47 = f32[2,8,2,64,512]{4,3,2,1,0:T(8,128)} custom-call(f32[8,2,33,8,128]{4,3,2,1,0:T(8,128)S(1)} %get-tuple-element.8.landed, f32[2,2,9,8,128]{4,3,2,1,0:T(8,128)S(1)} %get-tuple-element.9.values, f32[2,2,8,512]{3,2,1,0:T(8,128)S(1)} %get-tuple-element.10.cols), custom_call_target="tpu_custom_call" | custom-call | tf_op jit(solution)/shard_map/pallas_call | solution.py:586

commit v3 on v2

--- a/solution.py
+++ b/solution.py
@@ -80,8 +80,8 @@
 
 def solve_kernel(
     dims, slot_in, edge_in, forcing, inverse, landed, values_landed, cols,
-    slot, edge, raw, blocks_in, even_src, odd_src, part, stash, weighed, packed, ends, everyone,
-    uvals, values,
+    slot, edge, raw, blocks_in, even_src, odd_src, part, stash, weighed, packed, lefts, ends,
+    everyone, uvals, values,
     small_sem, raw_sem, in_sem, w_sem, z_send, z_recv, p_sem, u_sem, f_sem,
 ):
     fields, points, degrees, group, subs, groups = dims
@@ -97,6 +97,10 @@
     pair = me + 1 - 2 * parity
     far = groups - 2
     middle = groups - 4
+    size = group * tiles
+    mine = blocks // 2
+    own_blocks = pl.ds(parity * mine, mine)
+    its_blocks = pl.ds((1 - parity) * mine, mine)
     spot_left, spot_influence = tiles, tiles + 1
 
     def other(k):
@@ -105,48 +109,53 @@
     def late_mask(j):
         return 2 + (middle // 2) * (1 - lax.rem(j, 2)) + j // 2
 
-    def fetch(k, f):
-        index = 0
-        if isinstance(k, int) and k >= far:
-            index = k - far + 1
+    def fetch(k, f, which, n):
         return pltpu.make_async_copy(
-            inverse.at[0, f, pl.ds(other(k) * group, group)],
-            blocks_in.at[k, f],
-            in_sem.at[index, f],
+            inverse.at[0, f, pl.ds(other(k) * group, group), which],
+            blocks_in.at[k, f, :, which],
+            in_sem.at[n],
         )
 
-    def rest_arrives(f):
-        most = blocks_in.at[pl.ds(0, far), f]
-        pltpu.make_async_copy(most, most, in_sem.at[0, f]).wait()
+    def arrived(count, f, which, n):
+        target = blocks_in.at[pl.ds(0, count), f, :, which]
+        pltpu.make_async_copy(target, target, in_sem.at[n]).wait()
+
+    everything = pl.ds(0, blocks)
 
     def load(f, h):
         part_q = pl.ds(h * (points // 2), points // 2)
         return pltpu.make_async_copy(forcing.at[f, part_q], raw.at[f, part_q], raw_sem.at[f, h])
 
-    def send(k, f):
+    def send(k, f, begin=0, end=None):
+        if end is None:
+            end = size + (f == fields - 1)
+        rows = pl.ds(f * size + begin, end - begin)
         return pltpu.make_async_remote_copy(
-            src_ref=packed.at[k, f], dst_ref=landed.at[k, f],
+            src_ref=packed.at[k, rows], dst_ref=landed.at[k, rows],
             send_sem=p_sem.at[0], recv_sem=p_sem.at[1],
             device_id=(sub, other(k)), device_id_type=MESH,
         )
 
+    def value_rows(f):
+        return pl.ds(f * 2 * tiles, 2 * tiles + (f == fields - 1))
+
     def send_values(f):
         return pltpu.make_async_remote_copy(
-            src_ref=values.at[f], dst_ref=values_landed.at[0, f],
+            src_ref=values.at[value_rows(f)], dst_ref=values_landed.at[0, value_rows(f)],
             send_sem=u_sem.at[0, f], recv_sem=u_sem.at[1, f],
             device_id=(sub, other(far)), device_id_type=MESH,
         )
 
     def forward(f):
         return pltpu.make_async_remote_copy(
-            src_ref=values_landed.at[0, f], dst_ref=values_landed.at[1, f],
+            src_ref=values_landed.at[0, value_rows(f)], dst_ref=values_landed.at[1, value_rows(f)],
             send_sem=f_sem.at[0, f], recv_sem=f_sem.at[1, f],
             device_id=(sub, pair), device_id_type=MESH,
         )
 
     load(0, 0).start()
     load(0, 1).start()
-    fetch(far, 0).start()
+    fetch(far + 1, 0, everything, 0).start()
     slot_copy = pltpu.make_async_copy(slot_in, slot, small_sem.at[0])
     edge_copy = pltpu.make_async_copy(edge_in, edge, small_sem.at[1])
     slot_copy.start()
@@ -157,7 +166,6 @@
         pl.semaphore_signal(barrier, inc=1, device_id=(to, me), device_id_type=MESH)
     for k in range(1, groups):
         pl.semaphore_signal(barrier, inc=1, device_id=(sub, other(k)), device_id_type=MESH)
-    fetch(far + 1, 0).start()
     slot_copy.wait()
     edge_copy.wait()
 
@@ -186,38 +194,42 @@
 
         lax.fori_loop(h * (points // 4), (h + 1) * (points // 4), two, 0)
 
-    def solve_half(k, f, into):
-        for t in range(tiles):
-            at = pl.ds(t * LANES, LANES)
-            both = t >= half
-
-            def step(n, sums, t=t, at=at, both=both):
-                sums = list(sums)
+    def solve_half(k, f, into, begin=0, end=group):
+        for span in (tuple(range(half)),) + tuple((t,) for t in range(half, tiles)):
+            units = [(p, t, 0) for t in span for p in range(begin, end)]
+            if span[0] >= half:
+                units += [(p, t, 1) for t in span for p in range(begin, end)]
+
+            def step(n, sums, span=span, units=units):
+                sums = dict(zip(units, sums))
                 for b in range(2):
                     block = 2 * n + b
                     for r in range(ROWS):
                         q = block * ROWS + r
-                        even = even_src[f, q, t]
-                        odd = odd_src[f, q, t - half] if both else None
-                        for p in range(group):
-                            line = blocks_in[k, f, p, block, pl.ds(r, 1), at]
-                            entry = jnp.broadcast_to(line, (ROWS, LANES))
-                            sums[p] += entry * even
-                            if both:
-                                sums[group + p] += entry * odd
-                return tuple(sums)
-
-            count = group * (2 if both else 1)
-            start = tuple(jnp.zeros((ROWS, LANES), F32) for _ in range(count))
+                        for t in span:
+                            even = even_src[f, q, t]
+                            odd = odd_src[f, q, t - half] if t >= half else None
+                            for p in range(begin, end):
+                                line = blocks_in[
+                                    k, f, p, block, pl.ds(r, 1), pl.ds(t * LANES, LANES)
+                                ]
+                                entry = jnp.broadcast_to(line, (ROWS, LANES))
+                                sums[p, t, 0] += entry * even
+                                if t >= half:
+                                    sums[p, t, 1] += entry * odd
+                return tuple(sums[unit] for unit in units)
+
+            start = tuple(jnp.zeros((ROWS, LANES), F32) for _ in units)
             sums = lax.fori_loop(0, blocks // 2, step, start)
-            for p in range(group):
-                into[p, t] = sums[p]
-                if both:
-                    into[p, tiles + t - half] = sums[group + p]
-
-    def write_half(k, f, source, dest, fold):
-        left = jnp.where(lane == MARK, m.astype(F32), 0.0)
-        for p in range(group):
+            for (p, t, o), total in zip(units, sums):
+                into[p, t + half * o] = total
+
+    def write_half(k, f, source, dest, fold, begin=0, end=group):
+        if f == 0 and begin == 0:
+            left = jnp.where(lane == MARK, m.astype(F32), 0.0)
+        else:
+            left = lefts[k]
+        for p in range(begin, end):
             full = [source[p, t] for t in range(wide)]
             if fold:
                 for t in range(tiles):
@@ -231,17 +243,17 @@
                         full[n] = full[n] + uvals[f, 1, n] * top
             pieces, spare = pack(full, m, degrees)
             for t in range(tiles):
-                dest[p * tiles + t] = pieces[t]
-            left = jnp.where(lane == p, spare, left)
-        dest[group * tiles] = left
+                dest[f * size + p * tiles + t] = pieces[t]
+            left = jnp.where(lane == f * group + p, spare, left)
+        if f == fields - 1 and end == group:
+            dest[fields * size] = left
+        else:
+            lefts[k] = left
 
     def early(k, f):
-        fetch(k, f).wait()
         solve_half(k, f, part)
-        write_half(k, f, part, packed.at[k, f], False)
-
-    mine = blocks // 2
-    own_blocks = parity * mine
+        write_half(k, f, part, packed.at[k], False)
+        send(k, f).start()
 
     def weigh(f):
         def add(k, sums):
@@ -251,7 +263,8 @@
                 top = edge[0, 1, other(k) * group + p]
                 for b in range(mine):
                     for t in range(tiles):
-                        entry = blocks_in[k, f, p, own_blocks + b, :, pl.ds(t * LANES, LANES)]
+                        at = parity * mine + b
+                        entry = blocks_in[k, f, p, at, :, pl.ds(t * LANES, LANES)]
                         n = b * tiles + t
                         sums[n] += low * entry
                         sums[mine * tiles + n] += top * entry
@@ -262,10 +275,10 @@
         for e in range(2):
             for b in range(mine):
                 for t in range(tiles):
-                    weighed[f, own_blocks + b, e, t] = sums[(e * mine + b) * tiles + t]
+                    weighed[f, parity * mine + b, e, t] = sums[(e * mine + b) * tiles + t]
 
     def swap(f):
-        shared = weighed.at[f, pl.ds(own_blocks, mine)]
+        shared = weighed.at[f, own_blocks]
         return pltpu.make_async_remote_copy(
             src_ref=shared, dst_ref=shared, send_sem=w_sem.at[0, f], recv_sem=w_sem.at[1, f],
             device_id=(sub, pair), device_id_type=MESH,
@@ -359,15 +372,15 @@
                 upper_value = jnp.where(sub == k, later, upper_value)
             lower.append(lower_value)
             upper.append(upper_value)
-        spares = jnp.zeros((ROWS, LANES), F32)
+        spares = values[fields * 2 * tiles] if f else jnp.zeros((ROWS, LANES), F32)
         for e, vector in enumerate((lower, upper)):
             for t in range(wide):
                 uvals[f, e, t] = vector[t]
             pieces, spare = pack(vector, m, degrees)
             for t in range(tiles):
-                values[f, e * tiles + t] = pieces[t]
-            spares = jnp.where(lane == e, spare, spares)
-        values[f, 2 * tiles] = spares
+                values[f * 2 * tiles + e * tiles + t] = pieces[t]
+            spares = jnp.where(lane == 2 * f + e, spare, spares)
+        values[fields * 2 * tiles] = spares
         send_values(f).start()
 
     def late_parts(j, f):
@@ -376,80 +389,76 @@
     def late_write(f):
         def one(j, _):
             k = late_mask(j)
-            write_half(k, f, stash.at[j], packed.at[k, f], True)
+            write_half(k, f, stash.at[j], packed.at[k], True)
             send(k, f).start()
             return 0
 
         lax.fori_loop(0, middle, one, 0)
 
     load(0, 0).wait()
-    load(1, 0).start()
-    load(1, 1).start()
+    for k in range(far + 1):
+        fetch(k, 0, own_blocks, 1).start()
     prepare(0, 0)
     load(0, 1).wait()
+    fetch(far, 0, its_blocks, 2).start()
+    prepare(0, 1)
+    fetch(far + 1, 0, everything, 0).wait()
     for k in range(far):
-        fetch(k, 0).start()
-    prepare(0, 1)
-    early(far, 0)
-    for k in (far, far + 1):
-        fetch(k, 1).start()
+        fetch(k, 0, its_blocks, 3).start()
+    for h in range(2):
+        load(1, h).start()
+    quarter = group // 2
+    solve_half(far + 1, 0, part, 0, quarter)
+    write_half(far + 1, 0, part, packed.at[far + 1], False, 0, quarter)
     pl.semaphore_wait(barrier, subs + groups - 2)
-    send(far, 0).start()
+    send(far + 1, 0, 0, quarter * tiles).start()
+    for k in (far + 1, far):
+        fetch(k, 1, everything, 4 + far + 1 - k).start()
+    solve_half(far + 1, 0, part, quarter, group)
+    write_half(far + 1, 0, part, packed.at[far + 1], False, quarter, group)
+    send(far + 1, 0, quarter * tiles).start()
+    arrived(far + 1, 0, own_blocks, 1)
     for k in range(far):
-        fetch(k, 1).start()
-    early(far + 1, 0)
-    send(far + 1, 0).start()
-    rest_arrives(0)
+        fetch(k, 1, everything, 6).start()
     weigh(0)
     swap(0).start()
+    fetch(far, 0, its_blocks, 2).wait()
+    early(far, 0)
+    swap(0).wait()
+    slopes(0)
     for h in range(2):
         load(1, h).wait()
         prepare(1, h)
+    fetch(far + 1, 1, everything, 4).wait()
+    early(far + 1, 1)
+    fetch(far, 1, everything, 5).wait()
     early(far, 1)
-    send(far, 1).start()
-    swap(0).wait()
-    slopes(0)
-    early(far + 1, 1)
-    send(far + 1, 1).start()
-    rest_arrives(1)
+    arrived(far, 0, its_blocks, 3)
+    arrived(far, 1, everything, 6)
     weigh(1)
     swap(1).start()
     late_parts(0, 0)
     swap(1).wait()
     slopes(1)
-
-    def more(f):
-        def one(j, _):
+    for f in range(fields):
+        def more(j, _, f=f):
             late_parts(j, f)
             return 0
 
-        lax.fori_loop(1 - f, middle, one, 0)
-
-    def turn(f, _):
-        more(f)
+        lax.fori_loop(1 if f == 0 else 0, middle, more, 0)
         interface(f)
         late_write(f)
-        return 0
-
-    lax.fori_loop(0, fields, turn, 0)
-
-    def to_pair(f, _):
+
+    for f in range(fields):
         solve_half(1, f, part)
-        write_half(1, f, part, packed.at[1, f], True)
+        write_half(1, f, part, packed.at[1], True)
         send(1, f).start()
-        return 0
-
-    lax.fori_loop(0, fields, to_pair, 0)
     for f in range(fields):
         send_values(f).wait_recv()
         forward(f).start()
-
-    def to_self(f, _):
+    for f in range(fields):
         solve_half(0, f, part)
-        write_half(0, f, part, landed.at[0, f], True)
-        return 0
-
-    lax.fori_loop(0, fields, to_self, 0)
+        write_half(0, f, part, landed.at[0], True)
     for f in range(fields):
         for p in range(group):
             cols[0, f, pl.ds(p, 1), :] = blocks_in[0, f, p, 0, pl.ds(0, 1), :]
@@ -480,17 +489,19 @@
         return pltpu.make_async_copy(out.at[k], result.at[:, :, :, rows, :], out_sem.at[k])
 
     def one(k, fold):
+        left = landed[k, fields * group * tiles]
+        m = spread(left, MARK).astype(jnp.int32)
         for f in range(fields):
-            left = landed[k, f, group * tiles]
-            m = spread(left, MARK).astype(jnp.int32)
             added = []
             for e in range(2 if fold else 0):
-                pieces = [values[k - far, f, e * tiles + t] for t in range(tiles)]
-                spare = spread(values[k - far, f, 2 * tiles], e)
+                at = (2 * f + e) * tiles
+                pieces = [values[k - far, at + t] for t in range(tiles)]
+                spare = spread(values[k - far, fields * 2 * tiles], 2 * f + e)
                 added.append(unpack(pieces, spare, m, degrees))
             for p in range(group):
-                pieces = [landed[k, f, p * tiles + t] for t in range(tiles)]
-                full = unpack(pieces, spread(left, p), m, degrees)
+                n = f * group + p
+                pieces = [landed[k, n * tiles + t] for t in range(tiles)]
+                full = unpack(pieces, spread(left, n), m, degrees)
                 for t in range(tiles):
                     at = pl.ds(t * LANES, LANES)
                     spots = (t,) if t < half else (t, t + half)
@@ -532,10 +543,10 @@
     half = tiles // 2
     wide = tiles + half
     assert halves == 2 and slots == ROWS and tiles == 4 and fields == 2
-    assert groups >= 8 and groups & (groups - 1) == 0 and group < MARK
-    count = group * tiles + 1
+    assert groups >= 8 and groups & (groups - 1) == 0 and fields * group < MARK
+    count = fields * group * tiles + 1
     end_count = tiles + 2
-    value_count = 2 * tiles + 1
+    value_count = fields * 2 * tiles + 1
     shape = jax.ShapeDtypeStruct
     blocks = points // ROWS
     dma = pltpu.SemaphoreType.DMA
@@ -544,8 +555,8 @@
         in_specs=[pl.BlockSpec(memory_space=pltpu.HBM)] * 4,
         out_specs=[pl.BlockSpec(memory_space=pltpu.VMEM)] * 3,
         out_shape=[
-            shape((groups, fields, count, ROWS, LANES), F32),
-            shape((2, fields, value_count, ROWS, LANES), F32),
+            shape((groups, count, ROWS, LANES), F32),
+            shape((2, value_count, ROWS, LANES), F32),
             shape((2, fields, group, degrees), F32),
         ],
         scratch_shapes=[
@@ -558,14 +569,15 @@
             pltpu.VMEM((group, wide, ROWS, LANES), F32),
             pltpu.VMEM((groups - 4, group, wide, ROWS, LANES), F32),
             pltpu.VMEM((fields, blocks, 2, tiles, ROWS, LANES), F32),
-            pltpu.VMEM((groups, fields, count, ROWS, LANES), F32),
+            pltpu.VMEM((groups, count, ROWS, LANES), F32),
+            pltpu.VMEM((groups, ROWS, LANES), F32),
             pltpu.VMEM((fields, 2, end_count, ROWS, LANES), F32),
             pltpu.VMEM((subs, fields, 2, end_count, ROWS, LANES), F32),
             pltpu.VMEM((fields, 2, wide, ROWS, LANES), F32),
-            pltpu.VMEM((fields, value_count, ROWS, LANES), F32),
+            pltpu.VMEM((value_count, ROWS, LANES), F32),
             dma((2,)),
             dma((fields, 2)),
-            dma((3, fields)),
+            dma((7,)),
             dma((2, fields)),
             dma((subs - 1, fields)),
             dma((subs - 1, fields)),

time: 35.7 us -> 35.3 us (0.989)
  Pallas kernels: 35.5 us -> 35.1 us
    pallas_call x1, Pallas kernels: 33 us -> 32.5 us  [body(): pl.pallas_call(functools.partial(solve_kernel, (fields, points, degrees,...]
where the time goes in v3:
time: 35.3 us; the launch traced here: 35.2 us
  Pallas kernels  35.1 us (99%)
    pallas_call x1, Pallas kernels, body(): pl.pallas_call(functools.partial(solve_kernel, (fields, points, degrees,...  32.5 us
    pallas_call x1, Pallas kernels, body(): pl.pallas_call(functools.partial(finish_kernel, (fields, degrees, group,...  2.6 us

profile of v3, /device:TPU:0, one launch (start us, length us, event | category | flops | bytes accessed | tf_op | source)
XLA Modules:
  0.0 35.2 jit_solution(14918847496167791448)
XLA Ops:
  0.0 32.5 %shard_map.46 = (f32[8,65,8,128]{3,2,1,0:T(8,128)S(1)}, f32[2,17,8,128]{3,2,1,0:T(8,128)S(1)}, f32[2,2,8,512]{3,2,1,0:T(8,128)S(1)}) custom-call(s32[8]{0:T(128)} %slot_in.1, f32[1,2,64]{2,1,0:T(2,128)} %edge_in.1, f32[2,64,2,8,512]{4,3,2,1,0:T(8,128)} %forcing.1, f32[1,2,64,8,8,512]{5,4,3,2,1,0:T(8,128)} %bitcast.1), custom_call_target="tpu_custom_call" | custom-call | tf_op jit(solution)/shard_map/pallas_call | solution.py:553
  32.6 2.6 %shard_map.47 = f32[2,8,2,64,512]{4,3,2,1,0:T(8,128)} custom-call(f32[8,65,8,128]{3,2,1,0:T(8,128)S(1)} %get-tuple-element.8.landed, f32[2,17,8,128]{3,2,1,0:T(8,128)S(1)} %get-tuple-element.9.values, f32[2,2,8,512]{3,2,1,0:T(8,128)S(1)} %get-tuple-element.10.cols), custom_call_target="tpu_custom_call" | custom-call | tf_op jit(solution)/shard_map/pallas_call | solution.py:598

commit v4 on v3

--- a/solution.py
+++ b/solution.py
@@ -83,6 +83,7 @@
     slot, edge, raw, blocks_in, even_src, odd_src, part, stash, weighed, packed, lefts, ends,
     everyone, uvals, values,
     small_sem, raw_sem, in_sem, w_sem, z_send, z_recv, p_sem, u_sem, f_sem,
+    ready,
 ):
     fields, points, degrees, group, subs, groups = dims
     tiles = degrees // LANES
@@ -162,8 +163,11 @@
     edge_copy.start()
     barrier = pltpu.get_barrier_semaphore()
     subs_to = [lax.rem(sub + n, subs) for n in range(1, subs)]
-    for to in subs_to:
-        pl.semaphore_signal(barrier, inc=1, device_id=(to, me), device_id_type=MESH)
+    for n in range(1, subs):
+        @pl.when(sub + n < subs)
+        def _(n=n):
+            above = lax.rem(sub + n, subs)
+            pl.semaphore_signal(barrier, inc=1, device_id=(above, me), device_id_type=MESH)
     for k in range(1, groups):
         pl.semaphore_signal(barrier, inc=1, device_id=(sub, other(k)), device_id_type=MESH)
     slot_copy.wait()
@@ -410,8 +414,13 @@
     quarter = group // 2
     solve_half(far + 1, 0, part, 0, quarter)
     write_half(far + 1, 0, part, packed.at[far + 1], False, 0, quarter)
-    pl.semaphore_wait(barrier, subs + groups - 2)
+    pl.semaphore_wait(barrier, groups - 1 + sub)
     send(far + 1, 0, 0, quarter * tiles).start()
+    for n in range(1, subs):
+        @pl.when(sub >= n)
+        def _(n=n):
+            below = lax.rem(sub + subs - n, subs)
+            pl.semaphore_signal(ready, inc=1, device_id=(below, me), device_id_type=MESH)
     for k in (far + 1, far):
         fetch(k, 1, everything, 4 + far + 1 - k).start()
     solve_half(far + 1, 0, part, quarter, group)
@@ -425,6 +434,11 @@
     fetch(far, 0, its_blocks, 2).wait()
     early(far, 0)
     swap(0).wait()
+
+    @pl.when(sub < subs - 1)
+    def _():
+        pl.semaphore_wait(ready, subs - 1 - sub)
+
     slopes(0)
     for h in range(2):
         load(1, h).wait()
@@ -584,6 +598,7 @@
             dma((2,)),
             dma((2, fields)),
             dma((2, fields)),
+            pltpu.SemaphoreType.REGULAR,
         ],
         compiler_params=pltpu.CompilerParams(
             collective_id=0, has_side_effects=True, vmem_limit_bytes=VMEM_BYTES

time: 35.3 us -> 34.4 us (0.975)
  Pallas kernels: 35.1 us -> 34.3 us
    pallas_call x1, Pallas kernels: 32.5 us -> 31.7 us  [body(): pl.pallas_call(functools.partial(solve_kernel, (fields, points, degrees,...]
where the time goes in v4:
time: 34.4 us; the launch traced here: 34.3 us
  Pallas kernels  34.3 us (100%)
    pallas_call x1, Pallas kernels, body(): pl.pallas_call(functools.partial(solve_kernel, (fields, points, degrees,...  31.7 us
    pallas_call x1, Pallas kernels, body(): pl.pallas_call(functools.partial(finish_kernel, (fields, degrees, group,...  2.6 us

profile of v4, /device:TPU:0, one launch (start us, length us, event | category | flops | bytes accessed | tf_op | source)
XLA Modules:
  0.0 34.3 jit_solution(3842963553983340877)
XLA Ops:
  0.0 31.7 %shard_map.46 = (f32[8,65,8,128]{3,2,1,0:T(8,128)S(1)}, f32[2,17,8,128]{3,2,1,0:T(8,128)S(1)}, f32[2,2,8,512]{3,2,1,0:T(8,128)S(1)}) custom-call(s32[8]{0:T(128)} %slot_in.1, f32[1,2,64]{2,1,0:T(2,128)} %edge_in.1, f32[2,64,2,8,512]{4,3,2,1,0:T(8,128)} %forcing.1, f32[1,2,64,8,8,512]{5,4,3,2,1,0:T(8,128)} %bitcast.1), custom_call_target="tpu_custom_call" | custom-call | tf_op jit(solution)/shard_map/pallas_call | solution.py:567
  31.7 2.6 %shard_map.47 = f32[2,8,2,64,512]{4,3,2,1,0:T(8,128)} custom-call(f32[8,65,8,128]{3,2,1,0:T(8,128)S(1)} %get-tuple-element.8.landed, f32[2,17,8,128]{3,2,1,0:T(8,128)S(1)} %get-tuple-element.9.values, f32[2,2,8,512]{3,2,1,0:T(8,128)S(1)} %get-tuple-element.10.cols), custom_call_target="tpu_custom_call" | custom-call | tf_op jit(solution)/shard_map/pallas_call | solution.py:613

commit v5 on v4

--- a/solution.py
+++ b/solution.py
@@ -76,6 +76,14 @@
         pieces[3],
     ]
     return even + odd
+
+
+def value_row(f, e, fields, tiles):
+    return (2 * f + e) * tiles + (e if f == fields - 1 else 0)
+
+
+def spare_row(fields, tiles):
+    return (2 * fields - 1) * tiles
 
 
 def solve_kernel(
@@ -137,22 +145,35 @@
             device_id=(sub, other(k)), device_id_type=MESH,
         )
 
-    def value_rows(f):
-        return pl.ds(f * 2 * tiles, 2 * tiles + (f == fields - 1))
-
-    def send_values(f):
-        return pltpu.make_async_remote_copy(
-            src_ref=values.at[value_rows(f)], dst_ref=values_landed.at[0, value_rows(f)],
-            send_sem=u_sem.at[0, f], recv_sem=u_sem.at[1, f],
-            device_id=(sub, other(far)), device_id_type=MESH,
-        )
-
-    def forward(f):
-        return pltpu.make_async_remote_copy(
-            src_ref=values_landed.at[0, value_rows(f)], dst_ref=values_landed.at[1, value_rows(f)],
-            send_sem=f_sem.at[0, f], recv_sem=f_sem.at[1, f],
-            device_id=(sub, pair), device_id_type=MESH,
-        )
+    def send_values(f, begin):
+        two_sided(f, begin, values, values_landed.at[0], u_sem, other(far))
+
+    def forward(f, begin):
+        two_sided(f, begin, values_landed.at[0], values_landed.at[1], f_sem, pair)
+
+    def two_sided(f, begin, source, dest, sem, to):
+        outer = (sub == 0) | (sub == subs - 1)
+        more = f == fields - 1
+        skip = (1 - lax.min(sub, 1)) * tiles
+        inner_rows = pl.ds(f * 2 * tiles, 2 * tiles + more)
+        outer_rows = pl.ds(f * 2 * tiles + skip, tiles + more)
+        for case, rows in ((outer, outer_rows), (jnp.logical_not(outer), inner_rows)):
+            copy = pltpu.make_async_remote_copy(
+                src_ref=source.at[rows], dst_ref=dest.at[rows],
+                send_sem=sem.at[0, f], recv_sem=sem.at[1, f],
+                device_id=(sub, to), device_id_type=MESH,
+            )
+
+            @pl.when(case)
+            def _(copy=copy):
+                begin(copy)
+
+    def clear(e):
+        for f in range(fields):
+            for slot_of in range(2):
+                for t in range(tiles):
+                    at = value_row(f, e, fields, tiles) + t
+                    values_landed[slot_of, at] = jnp.zeros((ROWS, LANES), F32)
 
     load(0, 0).start()
     load(0, 1).start()
@@ -162,6 +183,15 @@
     slot_copy.start()
     edge_copy.start()
     barrier = pltpu.get_barrier_semaphore()
+
+    @pl.when(sub == 0)
+    def _():
+        clear(0)
+
+    @pl.when(sub == subs - 1)
+    def _():
+        clear(1)
+
     subs_to = [lax.rem(sub + n, subs) for n in range(1, subs)]
     for n in range(1, subs):
         @pl.when(sub + n < subs)
@@ -376,28 +406,28 @@
                 upper_value = jnp.where(sub == k, later, upper_value)
             lower.append(lower_value)
             upper.append(upper_value)
-        spares = values[fields * 2 * tiles] if f else jnp.zeros((ROWS, LANES), F32)
+        spares = values[spare_row(fields, tiles)] if f else jnp.zeros((ROWS, LANES), F32)
         for e, vector in enumerate((lower, upper)):
             for t in range(wide):
                 uvals[f, e, t] = vector[t]
             pieces, spare = pack(vector, m, degrees)
             for t in range(tiles):
-                values[f * 2 * tiles + e * tiles + t] = pieces[t]
+                values[value_row(f, e, fields, tiles) + t] = pieces[t]
             spares = jnp.where(lane == 2 * f + e, spare, spares)
-        values[fields * 2 * tiles] = spares
-        send_values(f).start()
+        values[spare_row(fields, tiles)] = spares
+        send_values(f, lambda copy: copy.start())
 
     def late_parts(j, f):
         solve_half(late_mask(j), f, stash.at[j])
 
-    def late_write(f):
+    def late_write(f, count):
         def one(j, _):
             k = late_mask(j)
             write_half(k, f, stash.at[j], packed.at[k], True)
             send(k, f).start()
             return 0
 
-        lax.fori_loop(0, middle, one, 0)
+        lax.fori_loop(0, count, one, 0)
 
     load(0, 0).wait()
     for k in range(far + 1):
@@ -459,17 +489,23 @@
             late_parts(j, f)
             return 0
 
-        lax.fori_loop(1 if f == 0 else 0, middle, more, 0)
+        begin, end = (1, middle) if f == 0 else (0, middle - 1)
+        lax.fori_loop(begin, end, more, 0)
         interface(f)
-        late_write(f)
+        late_write(f, end)
+        for j in range(end, middle):
+            k = late_mask(j)
+            solve_half(k, f, part)
+            write_half(k, f, part, packed.at[k], True)
+            send(k, f).start()
 
     for f in range(fields):
         solve_half(1, f, part)
         write_half(1, f, part, packed.at[1], True)
         send(1, f).start()
     for f in range(fields):
-        send_values(f).wait_recv()
-        forward(f).start()
+        send_values(f, lambda copy: copy.wait_recv())
+        forward(f, lambda copy: copy.start())
     for f in range(fields):
         solve_half(0, f, part)
         write_half(0, f, part, landed.at[0], True)
@@ -478,8 +514,8 @@
             cols[0, f, pl.ds(p, 1), :] = blocks_in[0, f, p, 0, pl.ds(0, 1), :]
             cols[1, f, pl.ds(p, 1), :] = blocks_in[0, f, p, blocks - 1, pl.ds(ROWS - 1, 1), :]
     for f in range(fields):
-        send_values(f).wait_send()
-        forward(f).wait()
+        send_values(f, lambda copy: copy.wait_send())
+        forward(f, lambda copy: copy.wait())
     away = pl.ds(1, groups - 1)
     pltpu.make_async_remote_copy(
         src_ref=packed.at[away], dst_ref=landed.at[away],
@@ -508,9 +544,9 @@
         for f in range(fields):
             added = []
             for e in range(2 if fold else 0):
-                at = (2 * f + e) * tiles
+                at = value_row(f, e, fields, tiles)
                 pieces = [values[k - far, at + t] for t in range(tiles)]
-                spare = spread(values[k - far, fields * 2 * tiles], 2 * f + e)
+                spare = spread(values[k - far, spare_row(fields, tiles)], 2 * f + e)
                 added.append(unpack(pieces, spare, m, degrees))
             for p in range(group):
                 n = f * group + p

time: 34.4 us -> 33.7 us (0.980)
  Pallas kernels: 34.3 us -> 33.6 us
    pallas_call x1, Pallas kernels: 31.7 us -> 31 us  [body(): pl.pallas_call(functools.partial(solve_kernel, (fields, points, degrees,...]
where the time goes in v5:
time: 33.7 us; the launch traced here: 33.6 us
  Pallas kernels  33.6 us (100%)
    pallas_call x1, Pallas kernels, body(): pl.pallas_call(functools.partial(solve_kernel, (fields, points, degrees,...  31 us
    pallas_call x1, Pallas kernels, body(): pl.pallas_call(functools.partial(finish_kernel, (fields, degrees, group,...  2.61 us

profile of v5, /device:TPU:0, one launch (start us, length us, event | category | flops | bytes accessed | tf_op | source)
XLA Modules:
  0.0 33.6 jit_solution(7287508605981920915)
XLA Ops:
  0.0 31.0 %shard_map.46 = (f32[8,65,8,128]{3,2,1,0:T(8,128)S(1)}, f32[2,17,8,128]{3,2,1,0:T(8,128)S(1)}, f32[2,2,8,512]{3,2,1,0:T(8,128)S(1)}) custom-call(s32[8]{0:T(128)} %slot_in.1, f32[1,2,64]{2,1,0:T(2,128)} %edge_in.1, f32[2,64,2,8,512]{4,3,2,1,0:T(8,128)} %forcing.1, f32[1,2,64,8,8,512]{5,4,3,2,1,0:T(8,128)} %bitcast.1), custom_call_target="tpu_custom_call" | custom-call | tf_op jit(solution)/shard_map/pallas_call | solution.py:603
  31.0 2.6 %shard_map.47 = f32[2,8,2,64,512]{4,3,2,1,0:T(8,128)} custom-call(f32[8,65,8,128]{3,2,1,0:T(8,128)S(1)} %get-tuple-element.8.landed, f32[2,17,8,128]{3,2,1,0:T(8,128)S(1)} %get-tuple-element.9.values, f32[2,2,8,512]{3,2,1,0:T(8,128)S(1)} %get-tuple-element.10.cols), custom_call_target="tpu_custom_call" | custom-call | tf_op jit(solution)/shard_map/pallas_call | solution.py:649
